TPU v7x, 32 devices: a whole 2x2x4 slice. The times are simulated.
32 devices in a mesh: seq: 16 (over z, y, core), fsdp: 2 (over x).
Axes of the slice: x: 2, y: 2, z: 4, core: 2. Of those that a mesh axis runs over, the one named last changes fastest.
Arguments:
- tokens: bfloat16 [8192, 5376], P(('seq', 'fsdp')), may hold values from -6 to 6
- norm_gain: float32 [5376], replicated, may hold values from 0.1 to 1.9
- query_weight: bfloat16 [5376, 2048], P('seq', 'fsdp'), may hold values from -0.078125 to 0.078125
- key_matrix: bfloat16 [5376, 1024], P('seq', 'fsdp'), may hold values from -0.078125 to 0.078125
- value_matrix: bfloat16 [5376, 1024], P('seq', 'fsdp'), may hold values from -0.078125 to 0.078125
- out_weight: bfloat16 [5376, 2048], P('seq', 'fsdp'), may hold values from -0.125 to 0.125
- query_gain: float32 [128], replicated, may hold values from 0.1 to 1.9
- key_gain: float32 [128], replicated, may hold values from 0.1 to 1.9
- post_gain: float32 [5376], replicated, may hold values from 0.1 to 1.9
Outputs:
- layer_out: bfloat16 [8192, 5376], P(('seq', 'fsdp'))
All inputs are finite; a program needn't handle non-finite values.
Results may differ from a plain program's by a relative error of at most 0.011.
Values may be sent and summed in bfloat16 or wider, within the bound.
A program may use at most 192 MiB of HBM per device.

v0:
```python
import functools

import jax
import jax.numpy as jnp
from jax import lax
from jax.experimental import pallas as pl
from jax.experimental.pallas import tpu as pltpu
from jax.sharding import PartitionSpec as P

HEAD_SIZE = 128
WINDOW_LENGTH = 1024


epsilon = 1e-06
score_scale = 168.0 ** (-0.5)
rope_base = 10000.0
masked_score = -1e30


def passed_along(block, axis, distance):
    devices = range(lax.axis_size(axis))
    route = [(i - distance, i) for i in devices if i - distance in devices]
    return lax.ppermute(block, axis, route)


def rms_scaled(values, gain):
    mean_square = jnp.mean(values * values, axis=-1, keepdims=True)
    return values * lax.rsqrt(mean_square + epsilon) * gain


def rotary(values, positions):
    half_width = values.shape[-1] // 2
    exponents = jnp.arange(half_width, dtype=jnp.float32) * (2.0 / values.shape[-1])
    frequency = jnp.exp(-exponents * jnp.log(jnp.float32(rope_base)))
    angles = positions.astype(jnp.float32)[:, None] * frequency[None, :]
    cosine = jnp.cos(angles)[:, None, :]
    sine = jnp.sin(angles)[:, None, :]
    first_half = values[..., :half_width]
    second_half = values[..., half_width:]
    return jnp.concatenate(
        [first_half * cosine - second_half * sine, second_half * cosine + first_half * sine],
        axis=-1,
    )


def head_states(projected, gain, positions):
    shaped = projected.reshape(projected.shape[0], -1, HEAD_SIZE)
    return rotary(rms_scaled(shaped, gain), positions).astype(jnp.bfloat16)


def window_block(query_block, key_block, value_block, query_pos, key_pos):
    scores = (
        jnp.einsum("rkgd,lkd->kgrl", query_block, key_block, preferred_element_type=jnp.float32)
        * score_scale
    )
    offset = query_pos[:, None] - key_pos[None, :]
    allowed = (offset >= 0) & (offset < WINDOW_LENGTH) & (key_pos[None, :] >= 0)
    scores = jnp.where(allowed, scores, masked_score)
    highest = jnp.max(scores, axis=-1, keepdims=True)
    raised = jnp.exp(scores - highest)
    weights = (raised / jnp.sum(raised, axis=-1, keepdims=True)).astype(jnp.bfloat16)
    mixed = jnp.einsum("kgrl,lkd->rkgd", weights, value_block, preferred_element_type=jnp.float32)
    return mixed.astype(jnp.bfloat16).reshape(query_block.shape[0], -1)


def ring_place(chip, chips):
    row, side = chip // 2, chip % 2
    return side * (chips - 1 - row) + (1 - side) * row


def ring_chip(place, chips):
    back = place // (chips // 2)
    return back * (2 * (chips - 1 - place) + 1) + (1 - back) * 2 * place


def gather_kernel(
    shards,
    copies,
    query_ref,
    key_ref,
    value_ref,
    tokens_ref,
    query_out,
    key_out,
    value_out,
    tokens_out,
    local_sem,
    ring_send,
    ring_recv,
    pair_send,
    pair_recv,
    token_send,
    token_recv,
):
    chips = shards // 2
    me = lax.axis_index("seq")
    group = lax.axis_index("fsdp")
    core = me % 2
    place = ring_place(me // 2, chips)
    half = query_ref.shape[1] // 2
    other = (me // 2) * 2 + 1 - core
    ahead = ring_chip((place + 1) % chips, chips) * 2 + core
    behind = ring_chip((place + chips - 1) % chips, chips) * 2 + core

    barrier = pltpu.get_barrier_semaphore()
    for device in (other, ahead, behind):
        pl.semaphore_signal(
            barrier, inc=1, device_id=(device, group), device_id_type=pl.DeviceIdType.MESH
        )
    for offset in range(1, copies):
        pl.semaphore_signal(
            barrier,
            inc=1,
            device_id=(me, (group + offset) % copies),
            device_id_type=pl.DeviceIdType.MESH,
        )
    pl.semaphore_wait(barrier, 3 + copies - 1)

    flows = (
        (query_ref, query_out, 0, half, 1),
        (key_ref, key_out, 0, key_ref.shape[1], -1),
        (query_ref, query_out, half, half, 1),
        (value_ref, value_out, 0, value_ref.shape[1], -1),
    )
    pending = []
    arriving = []
    token_slot = tokens_out.at[group]
    ring_copies = {}
    for step in range(chips):
        for index, (source, target, column, width, way) in enumerate(flows):
            columns = pl.ds(column, width)
            owner = ring_chip((place - way * step + chips) % chips, chips) * 2 + core
            slot = target.at[owner, :, columns]
            if step == 0:
                block = source.at[:, columns]
            else:
                block = slot
                ring_copies[index, step - 1].wait_recv()
            if step < chips - 1:
                copy = pltpu.make_async_remote_copy(
                    src_ref=block,
                    dst_ref=slot,
                    send_sem=ring_send.at[index, step],
                    recv_sem=ring_recv.at[index, step],
                    device_id=(ahead if way > 0 else behind, group),
                    device_id_type=pl.DeviceIdType.MESH,
                )
                copy.start()
                ring_copies[index, step] = copy
                pending.append(copy)
            across = pltpu.make_async_remote_copy(
                src_ref=block,
                dst_ref=slot,
                send_sem=pair_send.at[index, step],
                recv_sem=pair_recv.at[index, step],
                device_id=(other, group),
                device_id_type=pl.DeviceIdType.MESH,
            )
            across.start()
            pending.append(across)
            arriving.append(across)
        if step == 0:
            for offset in range(1, copies):
                swap = pltpu.make_async_remote_copy(
                    src_ref=tokens_ref,
                    dst_ref=token_slot,
                    send_sem=token_send.at[offset - 1],
                    recv_sem=token_recv.at[offset - 1],
                    device_id=(me, (group + offset) % copies),
                    device_id_type=pl.DeviceIdType.MESH,
                )
                swap.start()
                pending.append(swap)
                arriving.append(swap)
            local = [
                pltpu.make_async_copy(query_ref, query_out.at[me], local_sem.at[0]),
                pltpu.make_async_copy(key_ref, key_out.at[me], local_sem.at[1]),
                pltpu.make_async_copy(value_ref, value_out.at[me], local_sem.at[2]),
                pltpu.make_async_copy(tokens_ref, token_slot, local_sem.at[3]),
            ]
            for copy in local:
                copy.start()
    for copy in arriving:
        copy.wait_recv()
    for copy in pending:
        copy.wait_send()
    for copy in local:
        copy.wait()


def gathered(query_weight, key_matrix, value_matrix, tokens):
    shards, copies = lax.axis_size("seq"), lax.axis_size("fsdp")
    inputs = (query_weight, key_matrix, value_matrix, tokens)
    counts = (shards, shards, shards, copies)
    outputs = [
        jax.ShapeDtypeStruct((n, *a.shape), a.dtype) for a, n in zip(inputs, counts)
    ]
    chips = shards // 2
    anywhere = pl.BlockSpec(memory_space=pltpu.MemorySpace.HBM)
    whole = pl.pallas_call(
        functools.partial(gather_kernel, shards, copies),
        out_shape=outputs,
        in_specs=[anywhere] * 4,
        out_specs=[anywhere] * 4,
        scratch_shapes=[
            pltpu.SemaphoreType.DMA((4,)),
            pltpu.SemaphoreType.DMA((4, chips)),
            pltpu.SemaphoreType.DMA((4, chips)),
            pltpu.SemaphoreType.DMA((4, chips)),
            pltpu.SemaphoreType.DMA((4, chips)),
            pltpu.SemaphoreType.DMA((copies,)),
            pltpu.SemaphoreType.DMA((copies,)),
        ],
        compiler_params=pltpu.CompilerParams(collective_id=0, has_side_effects=True),
    )(*inputs)
    return [a.reshape(-1, a.shape[-1]) for a in whole]


def on_device(
    tokens,
    norm_gain,
    query_weight,
    key_matrix,
    value_matrix,
    out_weight,
    query_gain,
    key_gain,
    post_gain,
):
    query_full, key_full, value_full, pair_rows = gathered(
        query_weight, key_matrix, value_matrix, tokens
    )
    out_weight, pair_rows = lax.optimization_barrier((out_weight, pair_rows))
    out_full = lax.all_gather(out_weight, "seq", axis=0, tiled=True)
    shard_rows = pair_rows.shape[0]
    first_row = lax.axis_index("seq") * shard_rows
    normed_input = rms_scaled(pair_rows.astype(jnp.float32), norm_gain).astype(jnp.bfloat16)
    query_width = query_weight.shape[1]
    key_width = key_matrix.shape[1]
    local_heads = key_width // HEAD_SIZE
    query_groups = query_width // key_width
    keys_raw = jnp.dot(normed_input, key_full, preferred_element_type=jnp.float32)
    values_raw = jnp.dot(normed_input, value_full, preferred_element_type=jnp.float32)
    queries_raw = jnp.dot(normed_input, query_full, preferred_element_type=jnp.float32)
    positions = first_row + jnp.arange(shard_rows, dtype=jnp.int32)
    query_states = head_states(queries_raw, query_gain, positions).reshape(
        shard_rows, local_heads, query_groups, HEAD_SIZE
    )
    keys_now = head_states(keys_raw, key_gain, positions).reshape(shard_rows, key_width)
    values_now = values_raw.astype(jnp.bfloat16)
    stacked = jnp.stack([keys_now, values_now])
    reach = min(WINDOW_LENGTH, shard_rows)
    count = WINDOW_LENGTH // reach
    received = []
    for distance in range(1, count + 1):
        received = [passed_along(stacked, "seq", distance)] + received
    window_rows = jnp.concatenate(received + [stacked], axis=1)
    copies = lax.axis_size("fsdp")
    group = lax.axis_index("fsdp")
    part_rows = shard_rows // copies
    part_keys = window_rows.shape[1] - shard_rows + part_rows

    def partial_rows(part, states):
        begin = part * part_rows
        queries = lax.dynamic_slice_in_dim(states, begin, part_rows, 0)
        window = lax.dynamic_slice_in_dim(window_rows, begin, part_keys, 1)
        keys = window[0].reshape(part_keys, local_heads, HEAD_SIZE)
        values = window[1].reshape(part_keys, local_heads, HEAD_SIZE)
        query_pos = first_row + begin + jnp.arange(part_rows, dtype=jnp.int32)
        key_pos = first_row + begin - WINDOW_LENGTH + jnp.arange(part_keys, dtype=jnp.int32)
        attended = window_block(queries, keys, values, query_pos, key_pos)
        return lax.dot_general(
            attended, out_full, (((1,), (1,)), ((), ())), preferred_element_type=jnp.float32
        ).astype(jnp.bfloat16)

    summed = 0.0
    for offset in range(1, copies):
        away = partial_rows((group + offset) % copies, query_states)
        route = [(i, (i + offset) % copies) for i in range(copies)]
        query_states, away = lax.optimization_barrier((query_states, away))
        summed = summed + lax.ppermute(away, "fsdp", route).astype(jnp.float32)
    summed = partial_rows(group, query_states).astype(jnp.float32) + summed
    return (tokens.astype(jnp.float32) + rms_scaled(summed, post_gain)).astype(jnp.bfloat16)


def solution(mesh):
    in_specs = (
        P(("seq", "fsdp"), None),
        P(),
        P("seq", "fsdp"),
        P("seq", "fsdp"),
        P("seq", "fsdp"),
        P("seq", "fsdp"),
        P(),
        P(),
        P(),
    )
    out_specs = P(("seq", "fsdp"), None)
    return jax.shard_map(
        on_device, mesh=mesh, in_specs=in_specs, out_specs=out_specs, check_vma=False
    )
```

profile of v0, /device:TPU:5, one launch (start us, length us, event | category | flops | bytes accessed | tf_op | source)
XLA Modules:
  0.0 341.6 jit_solution(12876229470253224511)
XLA Ops:
  6.5 0.0 all-gather.2.cloned.1.call-start
  6.5 128.7 %shard_map.91 = (bf16[16,336,1024]{2,1,0:T(8,128)(2,1)}, bf16[16,336,512]{2,1,0:T(8,128)(2,1)}, bf16[16,336,512]{2,1,0:T(8,128)(2,1)}, bf16[2,256,5376]{2,1,0:T(8,128)(2,1)}) custom-call(bf16[336,1024]{1,0:T(8,128)(2,1)} %query_ref.1, bf16[336,512]{1,0:T(8,128)(2,1)} %key_ref.1, bf16[336,512]{1,0:T(8,128)(2,1)} %value_ref.1, bf16[256,5376]{1,0:T(8,128)(2,1)} %tokens_ref.1), custom_call_target="tpu_custom_call" | custom-call | tf_op jit(solution)/shard_map/pallas_call | solution.py:200
  135.2 0.0 all-gather.2.cloned.1.call-update
  135.3 0.0 copy-start.7
  135.3 8.3 %copy.10 = bf16[512,5376]{1,0:T(8,128)(2,1)} copy(bf16[512,5376]{0,1:T(8,128)(2,1)} %bitcast.81) | data formatting | bytes 11010048 | tf_op jit(solution)/shard_map/dot_general | solution.py:242
  143.6 0.0 copy-start.1
  143.6 4.3 %fusion.2 = f32[512]{0:T(512)S(1)} fusion(bf16[512,5376]{1,0:T(8,128)(2,1)} %bitcast.77), kind=kLoop, calls=%fused_computation.4 | loop fusion | flops 8257024 | bytes 5507072 | tf_op jit(solution)/shard_map/reduce_sum | solution.py:27
  147.9 0.0 copy-done.7
  147.9 0.3 copy-done.1
  148.3 0.0 copy-start.5
  148.3 5.4 %multiply_reduce_fusion.2 = (f32[512,4]{0,1:T(4,128)S(1)}, f32[512,4,128]{0,2,1:T(8,128)S(1)}) fusion(bf16[4,128,5376]{2,1,0:T(8,128)(2,1)S(1)} %bitcast.82, f32[5376]{0:T(1024)S(1)} %copy-done.7, f32[512]{0:T(512)S(1)} %add_rsqrt_fusion.2, bf16[512,5376]{1,0:T(8,128)(2,1)} %bitcast.78), kind=kOutput, calls=%fused_computation.56 | convolution fusion | flops 2830104576 | bytes 12090368 | tf_op jit(solution)/shard_map/dot_general | solution.py:242
  153.7 0.5 multiply_cosine_fusion
  154.2 0.0 copy-done.5
  154.3 0.2 multiply_multiply_fusion.1
  154.5 0.2 subtract_convert_fusion.1
  154.7 0.2 copy.11
  154.9 7.3 %fusion.30 = bf16[1,512,512]{2,1,0:T(8,128)(2,1)S(1)} fusion(bf16[5376,512]{1,0:T(8,128)(2,1)} %bitcast.92, bf16[512,5376]{1,0:T(8,128)(2,1)} %bitcast.79, f32[5376]{0:T(1024)S(1)} %copy-done.7, f32[512]{0:T(512)S(1)} %add_rsqrt_fusion.2), kind=kOutput, calls=%fused_computation.51 | convolution fusion | flops 2829844480 | bytes 11557888 | tf_op jit(solution)/shard_map/dot_general | solution.py:243
  162.2 1.1 pad_maximum_fusion
  163.3 3.8 %collective-permute-start.1 = (bf16[2,512,512]{2,1,0:T(8,128)(2,1)}, bf16[2,512,512]{2,1,0:T(8,128)(2,1)}, u32[]{:S(2)}, u32[]{:S(2)}) collective-permute-start(bf16[2,512,512]{2,1,0:T(8,128)(2,1)} %pad_maximum_fusion), channel_id=1, source_target_pairs={{0,2},{2,4},{4,6},{6,8},{8,10},{10,12},{12,14},{14,16},{16,18},{18... | collective-permute-start | bytes 3145736 | tf_op jit(solution)/shard_map/ppermute | solution.py:23
  167.1 3.3 collective-permute-start
  170.4 14.2 %copy.12 = bf16[1024,5376]{1,0:T(8,128)(2,1)} copy(bf16[1024,5376]{0,1:T(8,128)(2,1)} %bitcast.75) | data formatting | bytes 22020096 | tf_op jit(solution)/shard_map/dot_general | solution.py:244
  184.6 0.0 copy-start.6
  184.6 10.5 %multiply_reduce_fusion.1 = (f32[512,8]{0,1:T(8,128)S(1)}, f32[512,8,128]{0,2,1:T(8,128)S(1)}) fusion(bf16[8,128,5376]{2,1,0:T(8,128)(2,1)} %bitcast.76, f32[5376]{0:T(1024)S(1)} %copy-done.7, f32[512]{0:T(512)S(1)} %add_rsqrt_fusion.2, bf16[512,5376]{1,0:T(8,128)(2,1)} %bitcast.80), kind=kOutput, calls=%fused_computation.35 | convolution fusion | flops 5649199104 | bytes 18652160 | tf_op jit(solution)/shard_map/dot_general | solution.py:244
  195.1 0.0 copy-done.6
  195.1 0.5 multiply_multiply_fusion
  195.6 1.2 subtract_convert_fusion
  196.8 0.5 copy.14
  197.3 1.5 copy.13
  198.8 1.1 fusion.39
  200.0 1.6 pad_maximum_fusion.1
  201.6 0.9 fusion.27
  202.5 0.0 collective-permute-done.1
  202.5 30.3 %collective-permute-done = bf16[2,512,512]{2,1,0:T(8,128)(2,1)} collective-permute-done((bf16[2,512,512]{2,1,0:T(8,128)(2,1)}, bf16[2,512,512]{2,1,0:T(8,128)(2,1)}, u32[]{:S(2)}, u32[]{:S(2)}) %collective-permute-start) | collective-permute-done | bytes 1048608 | tf_op jit(solution)/shard_map/ppermute | solution.py:23
  232.8 1.7 maximum_maximum_fusion
  234.5 0.0 copy-start.3
  234.5 2.1 constant_dynamic-slice_fusion.2
  236.6 2.4 copy.30
  239.1 3.8 %reshape_squeeze.15 = bf16[1280,4,128]{2,1,0:T(4,128)(2,1)} reshape(bf16[1,1280,512]{2,1,0:T(8,128)(2,1)} %get-tuple-element.21) | data formatting | bytes 2621440 | tf_op jit(solution)/shard_map/reshape;squeeze | solution.py:267
  242.8 0.0 copy-done.3
  242.8 5.0 %fusion.84 = f32[4,2,256]{2,1,0:T(2,128)S(1)} fusion(pred[256,1280]{0,1:T(8,128)(4,1)S(1)} %fusion.27, bf16[256,4,2,128]{3,0,2,1:T(8,128)(2,1)S(1)} %copy-done.3, bf16[1280,4,128,1]{2,1,0,3:T(4,128)(2,1)} %bitcast.90), kind=kOutput, calls=%fused_computation.97 | convolution fusion | flops 681575680 | bytes 2170880 | tf_op jit(solution)/shard_map/sub | solution.py:60
  247.8 7.5 %fusion.29 = bf16[4,128,2,256]{3,1,2,0:T(8,128)(2,1)} fusion(bf16[1280,4,128,1]{0,2,3,1:T(8,128)(2,1)} %bitcast.87, f32[4,2,256]{2,1,0:T(2,128)S(1)} %fusion.84, pred[256,1280]{0,1:T(8,128)(4,1)S(1)} %fusion.27, bf16[256,4,2,128]{3,0,2,1:T(8,128)(2,1)S(1)} %copy-done.3, bf16[1280,4,128,1]{2,1,0,3:T(4,128)(2,1)} %bitcast.91), kind=kOutput, calls=%fused_computation.50 | convolution fusion | flops 1355549952 | bytes 4005888 | tf_op jit(solution)/shard_map/kgrl,lkd->rkgd/dot_general | solution.py:62
  255.3 0.0 all-gather.2.cloned.1.call-done
  255.3 8.9 %convolution_convert_fusion.1 = bf16[256,5376]{1,0:T(8,128)(2,1)} fusion(bf16[256,1024]{0,1:T(8,128)(2,1)} %bitcast.94, bf16[5376,1024]{1,0:T(8,128)(2,1)} %all-gather.2.cloned.1.call-done), kind=kOutput, calls=%fused_computation.17 | convolution fusion | flops 2819948544 | bytes 14286848 | tf_op jit(solution)/shard_map/dot_general | solution.py:272
  264.2 1.1 collective-permute-start.2
  265.4 1.0 fusion.25
  266.4 1.5 copy.27
  267.8 0.6 reshape_squeeze.13
  268.4 0.0 copy-start.2
  268.4 4.8 %fusion.87 = f32[4,2,256]{2,1,0:T(2,128)S(1)} fusion(pred[256,1280]{0,1:T(8,128)(4,1)S(1)} %fusion.25, bf16[1280,4,128,1]{2,1,0,3:T(4,128)(2,1)S(1)} %bitcast.88, bf16[512,4,2,128]{3,0,2,1:T(8,128)(2,1)} %pad_maximum_fusion.1, s32[]{:T(128)S(6)} %select_n.31), kind=kOutput, calls=%fused_computation.98 | convolution fusion | flops 681575680 | bytes 2170884 | tf_op jit(solution)/shard_map/sub | solution.py:60
  273.3 0.0 copy-done.2
  273.3 6.0 %fusion.28 = bf16[4,128,2,256]{3,1,2,0:T(8,128)(2,1)S(1)} fusion(bf16[1280,4,128,1]{0,2,3,1:T(8,128)(2,1)S(1)} %bitcast.86, f32[4,2,256]{2,1,0:T(2,128)S(1)} %fusion.87, pred[256,1280]{0,1:T(8,128)(4,1)S(1)} %fusion.25, bf16[1280,4,128,1]{2,1,0,3:T(4,128)(2,1)S(1)} %bitcast.89, bf16[512,4,2,128]{3,0,2,1:T(8,128)(2,1)} %pad_maximum_fusion.1, s32[]{:T(128)S(6)} %select_n.31), kind=kOutput, calls=%fused_computation.49 | convolution fusion | flops 1355549952 | bytes 4005892 | tf_op jit(solution)/shard_map/kgrl,lkd->rkgd/dot_general | solution.py:62
  279.3 42.0 %collective-permute-done.2 = bf16[256,5376]{1,0:T(8,128)(2,1)} collective-permute-done((bf16[256,5376]{1,0:T(8,128)(2,1)}, bf16[256,5376]{1,0:T(8,128)(2,1)}, u32[]{:S(2)}, u32[]{:S(2)}) %collective-permute-start.2) | collective-permute-done | bytes 2752544 | tf_op jit(solution)/shard_map/ppermute | solution.py:281
  321.3 0.0 copy-start
  321.3 0.0 copy-start.4
  321.3 8.5 %multiply_reduce_fusion = (f32[256]{0:T(256)S(1)}, f32[256,5376]{1,0:T(8,128)S(1)}) fusion(bf16[256,5376]{1,0:T(8,128)(2,1)} %collective-permute-done.2, bf16[256,1024]{0,1:T(8,128)(2,1)S(1)} %bitcast.93, bf16[5376,1024]{1,0:T(8,128)(2,1)} %all-gather.2.cloned.1.call-done), kind=kOutput, calls=%fused_computation.23 | convolution fusion | flops 2826829568 | bytes 19792896 | tf_op jit(solution)/shard_map/dot_general | solution.py:272
  329.8 0.0 copy-done
  329.8 0.0 copy-done.4
  329.8 4.5 %add_convert_fusion = bf16[256,5376]{1,0:T(8,128)(2,1)} fusion(bf16[256,5376]{1,0:T(8,128)(2,1)S(1)} %copy-done, f32[256,5376]{1,0:T(8,128)S(1)} %get-tuple-element.36, bf16[256,5376]{1,0:T(8,128)(2,1)} %collective-permute-done.2, f32[5376]{0:T(1024)S(1)} %copy-done.4, f32[256]{0:T(256)S(1)} %add_rsqrt_fusion.3), kind=kLoop, calls=%fused_computation.22 | loop fusion | flops 9633792 | bytes 13785088 | tf_op jit(solution)/shard_map/convert_element_type | solution.py:283
  (13 shorter events, 0.1 us)
Async XLA Ops:
  6.5 248.8 %all-gather.2.cloned.1.call-start = ((), (), s32[]{:S(2)}) async-start(), calls=%async_computation | async-start | bytes 11698176 | tf_op jit(solution)/shard_map/all_gather | solution.py:234
  135.3 12.7 %copy-start.7 = (f32[5376]{0:T(1024)S(1)}, f32[5376]{0:T(1024)}, u32[]{:S(2)}) copy-start(f32[5376]{0:T(1024)} %param.10) | copy-start | bytes 64516
  143.6 4.7 %copy-start.1 = (bf16[512,5376]{1,0:T(8,128)(2,1)S(1)}, bf16[512,5376]{1,0:T(8,128)(2,1)}, u32[]{:S(2)}) copy-start(bf16[512,5376]{1,0:T(8,128)(2,1)} %copy.10) | copy-start | bytes 16515076
  148.3 6.0 %copy-start.5 = (f32[128]{0:T(128)S(1)}, f32[128]{0:T(128)}, u32[]{:S(2)}) copy-start(f32[128]{0:T(128)} %param.16) | copy-start | bytes 1540
  163.3 39.2 %collective-permute-start.1 = (bf16[2,512,512]{2,1,0:T(8,128)(2,1)}, bf16[2,512,512]{2,1,0:T(8,128)(2,1)}, u32[]{:S(2)}, u32[]{:S(2)}) collective-permute-start(bf16[2,512,512]{2,1,0:T(8,128)(2,1)} %pad_maximum_fusion), channel_id=1, source_target_pairs={{0,2},{2,4},{4,6},{6,8},{8,10},{10,12},{12,14},{14,16},{16,18},{18... | collective-permute-start | bytes 3145736 | tf_op jit(solution)/shard_map/ppermute | solution.py:23
  167.1 65.8 %collective-permute-start = (bf16[2,512,512]{2,1,0:T(8,128)(2,1)}, bf16[2,512,512]{2,1,0:T(8,128)(2,1)}, u32[]{:S(2)}, u32[]{:S(2)}) collective-permute-start(bf16[2,512,512]{2,1,0:T(8,128)(2,1)} %pad_maximum_fusion), channel_id=1, source_target_pairs={{0,4},{2,6},{4,8},{6,10},{8,12},{10,14},{12,16},{14,18},{16,20},{1... | collective-permute-start | bytes 3145736 | tf_op jit(solution)/shard_map/ppermute | solution.py:23
  184.6 10.5 %copy-start.6 = (f32[128]{0:T(128)S(1)}, f32[128]{0:T(128)}, u32[]{:S(2)}) copy-start(f32[128]{0:T(128)} %param.15) | copy-start | bytes 1540
  234.5 8.3 %copy-start.3 = (bf16[256,4,2,128]{3,0,2,1:T(8,128)(2,1)S(1)}, bf16[256,4,2,128]{3,0,2,1:T(8,128)(2,1)}, u32[]{:S(2)}) copy-start(bf16[256,4,2,128]{3,0,2,1:T(8,128)(2,1)} %fusion.39) | copy-start | bytes 1572868
  264.2 57.1 %collective-permute-start.2 = (bf16[256,5376]{1,0:T(8,128)(2,1)}, bf16[256,5376]{1,0:T(8,128)(2,1)}, u32[]{:S(2)}, u32[]{:S(2)}) collective-permute-start(bf16[256,5376]{1,0:T(8,128)(2,1)} %convolution_convert_fusion.1), channel_id=1, source_target_pairs={{0,1},{1,0},{2,3},{3,2},{4,5},{5,4},{6,7},{7,6},{8,9},{9,8},{10,11... | collective-permute-start | bytes 8257544 | tf_op jit(solution)/shard_map/ppermute | solution.py:281
  268.4 4.8 %copy-start.2 = (bf16[1,1280,512]{1,2,0:T(8,128)(2,1)S(1)}, bf16[1,1280,512]{1,2,0:T(8,128)(2,1)}, u32[]{:S(2)}) copy-start(bf16[1,1280,512]{1,2,0:T(8,128)(2,1)} %copy.27) | copy-start | bytes 3932164
  321.3 8.5 %copy-start = (bf16[256,5376]{1,0:T(8,128)(2,1)S(1)}, bf16[256,5376]{1,0:T(8,128)(2,1)}, u32[]{:S(2)}) copy-start(bf16[256,5376]{1,0:T(8,128)(2,1)} %tokens_ref.1) | copy-start | bytes 8257540
  321.3 8.5 %copy-start.4 = (f32[5376]{0:T(1024)S(1)}, f32[5376]{0:T(1024)}, u32[]{:S(2)}) copy-start(f32[5376]{0:T(1024)} %param.17) | copy-start | bytes 64516
Sparse Core Ops, SparseCore 0:
  135.4 114.5 all-gather.1
where the time goes:
time: 349 us; the launch traced here: 342 us
  Pallas kernels  129 us (37%)
  waiting for transfers between devices  72.3 us (21%)
  matrix products  63.9 us (18%)
  local copies, waits for them, and re-layouts  35.4 us (10%)
  other arithmetic  18.9 us (5%)
  between operations  14.2 us (4%)
  starting transfers between devices  8.24 us (2%)
    pallas_call x1, Pallas kernels, gathered(): pl.pallas_call(functools.partial(gather_kernel, shards, copies), out_shap...  129 us
    ppermute x1, waiting for transfers between devices, on_device(): summed = summed + lax.ppermute(away, 'fsdp', route).astype(jnp.float32)  42 us
    ppermute x2, waiting for transfers between devices, passed_along(): return lax.ppermute(block, axis, route)  30.3 us
    dot_general x2, matrix products, partial_rows(): lax.dot_general(attended, out_full, (((1,), (1,)), ((), ())), preferred_e...  17.4 us
    dot_general x1, local copies, waits for them, and re-layouts, on_device(): jnp.dot(normed_input, query_full, preferred_element_type=jnp.float32)  14.2 us
    dot_general x2, matrix products, window_block(): jnp.einsum('kgrl,lkd->rkgd', weights, value_block, preferred_element_type...  13.5 us
    dot_general x1, matrix products, on_device(): jnp.dot(normed_input, query_full, preferred_element_type=jnp.float32)  10.5 us
    sub x2, matrix products, window_block(): raised = jnp.exp(scores - highest)  9.79 us
  transfers between devices with their start and end apart: 4, of which 2 were waited for; matrix products, arithmetic and copies ran while one was open for 28% of the time, Pallas kernels for 0%

commit v1 on v0

v1 whole, which is shorter than its diff:
```python
import functools

import jax
import jax.numpy as jnp
from jax import lax
from jax.experimental import pallas as pl
from jax.experimental.pallas import tpu as pltpu
from jax.sharding import PartitionSpec as P

HEAD_SIZE = 128
WINDOW_LENGTH = 1024

epsilon = 1e-06
score_scale = 168.0 ** (-0.5)
log2_e = 1.4426950408889634
rope_base = 10000.0
pieces = 2
token_pieces = 4
MESH = pl.DeviceIdType.MESH


def ring_place(chip, chips):
    row, side = chip // 2, chip % 2
    return side * (chips - 1 - row) + (1 - side) * row


def ring_chip(place, chips):
    back = place // (chips // 2)
    return back * (2 * (chips - 1 - place) + 1) + (1 - back) * 2 * place


class Ring:
    def __init__(self, shards, sems):
        self.chips = shards // 2
        self.me = lax.axis_index("seq")
        self.group = lax.axis_index("fsdp")
        self.core = self.me % 2
        self.place = ring_place(self.me // 2, self.chips)
        self.other = (self.me // 2) * 2 + 1 - self.core
        self.ahead = self.neighbour(1)
        self.behind = self.neighbour(self.chips - 1)
        self.ring_send, self.ring_recv, self.pair_send, self.pair_recv = sems

    def neighbour(self, distance):
        return ring_chip((self.place + distance) % self.chips, self.chips) * 2 + self.core

    def owner(self, way, step):
        return ring_chip((self.place + (self.chips - way) * step) % self.chips, self.chips)

    def ring_copy(self, flow, step):
        index, slot_of, way = flow
        slot = slot_of(self.owner(way, step), self.core)
        return pltpu.make_async_remote_copy(
            src_ref=slot,
            dst_ref=slot,
            send_sem=self.ring_send.at[index, step],
            recv_sem=self.ring_recv.at[index, step],
            device_id=(self.ahead if way > 0 else self.behind, self.group),
            device_id_type=MESH,
        )

    def arrival(self, flow, step):
        index, slot_of, way = flow
        slot = slot_of(self.owner(way, step), self.core)
        return pltpu.make_async_remote_copy(
            src_ref=slot,
            dst_ref=slot,
            send_sem=self.ring_send.at[index, step - 1],
            recv_sem=self.ring_recv.at[index, step - 1],
            device_id=(self.ahead if way > 0 else self.behind, self.group),
            device_id_type=MESH,
        )

    def pair_copy(self, flow, step, core):
        index, slot_of, way = flow
        slot = slot_of(self.owner(way, step), core)
        return pltpu.make_async_remote_copy(
            src_ref=slot,
            dst_ref=slot,
            send_sem=self.pair_send.at[index, step],
            recv_sem=self.pair_recv.at[index, step],
            device_id=(self.other, self.group),
            device_id_type=MESH,
        )

    def hop(self, flows, step, first=False, last=False):
        for flow in flows:
            if not first:
                self.arrival(flow, step).wait_recv()
            if not last:
                self.ring_copy(flow, step).start()
            self.pair_copy(flow, step, self.core).start()

    def landed(self, flows, step):
        for flow in flows:
            self.pair_copy(flow, step, 1 - self.core).wait_recv()

    def drain(self, flows):
        def one(step, carry):
            for flow in flows:
                self.ring_copy(flow, step).wait_send()
                self.pair_copy(flow, step, self.core).wait_send()
            return carry

        lax.fori_loop(0, self.chips - 1, one, 0)
        for flow in flows:
            self.pair_copy(flow, self.chips - 1, self.core).wait_send()


def turned(values, gain, cosine, sine, scale):
    mean_square = jnp.mean(values * values, axis=-1, keepdims=True)
    normed = values * lax.rsqrt(mean_square + epsilon) * gain
    swapped = pltpu.roll(normed, values.shape[-1] // 2, 1)
    return (normed * cosine + swapped * sine) * scale


def project_kernel(
    shards,
    merge,
    tokens_ref,
    gain_ref,
    query_ref,
    key_ref,
    value_ref,
    out_ref,
    query_gain_ref,
    key_gain_ref,
    cosine_ref,
    sine_ref,
    query_out,
    key_out,
    value_out,
    swap_out,
    query_land,
    key_land,
    value_land,
    raw,
    split,
    query_sum,
    key_sum,
    value_sum,
    key_own,
    value_own,
    ring_send,
    ring_recv,
    pair_send,
    pair_recv,
    local_sem,
    token_send,
    token_recv,
    swap_sem,
    far_send,
    far_recv,
    near_send,
    near_recv,
):
    ring = Ring(shards, (ring_send, ring_recv, pair_send, pair_recv))
    chips, me, group, core = ring.chips, ring.me, ring.group, ring.core
    rows = key_ref.shape[0]
    part_rows = tokens_ref.shape[0]
    width = key_ref.shape[1]
    half = query_ref.shape[1] // 2
    far_to = (me + 2) % shards
    far_from = (me + shards - 2) % shards

    barrier = pltpu.get_barrier_semaphore()
    for device in (ring.other, ring.ahead, ring.behind, far_to, far_from):
        pl.semaphore_signal(barrier, inc=1, device_id=(device, group), device_id_type=MESH)
    pl.semaphore_signal(barrier, inc=1, device_id=(me, 1 - group), device_id_type=MESH)

    @pl.when(core != group)
    def _():
        pl.semaphore_signal(
            barrier,
            inc=1,
            device_id=((me // 2) * 2 + group, core),
            device_id_type=MESH,
        )

    local = [
        pltpu.make_async_copy(key_ref, key_land.at[me], local_sem.at[0]),
        pltpu.make_async_copy(value_ref, value_land.at[me], local_sem.at[1]),
        pltpu.make_async_copy(query_ref, query_land.at[me], local_sem.at[2]),
        pltpu.make_async_copy(tokens_ref, raw.at[group], local_sem.at[3]),
    ]
    for copy in local:
        copy.start()
    pl.semaphore_wait(barrier, 6 + (core + group) % 2)

    def flow(index, land, column, count, way):
        return index, lambda chip, side: land.at[chip * 2 + side, :, pl.ds(column, count)], way

    size, wide = width // pieces, half // pieces
    first_flows, second_flows = [], []
    for piece in range(pieces):
        first_flows.append(flow(2 * piece, key_land, piece * size, size, 1))
        first_flows.append(flow(2 * piece + 1, value_land, piece * size, size, -1))
    for piece in range(pieces):
        base = 2 * (pieces + piece)
        second_flows.append(flow(base, query_land, piece * wide, wide, 1))
        second_flows.append(flow(base + 1, query_land, half + piece * wide, wide, -1))

    token_rows = part_rows // token_pieces

    def token_copy(piece, side):
        span = pl.ds(piece * token_rows, token_rows)
        return pltpu.make_async_remote_copy(
            src_ref=tokens_ref.at[span],
            dst_ref=raw.at[side, span],
            send_sem=token_send.at[piece],
            recv_sem=token_recv.at[piece],
            device_id=(me, 1 - group),
            device_id_type=MESH,
        )

    swap = pltpu.make_async_remote_copy(
        src_ref=out_ref,
        dst_ref=swap_out,
        send_sem=swap_sem.at[0],
        recv_sem=swap_sem.at[1],
        device_id=((me // 2) * 2 + group, core),
        device_id_type=MESH,
    )

    local[0].wait()
    local[1].wait()
    ring.hop(first_flows, 0, first=True)
    for piece in range(token_pieces):
        token_copy(piece, group).start()

    @pl.when(core != group)
    def _():
        swap.start()

    local[2].wait()
    local[3].wait()

    block = 16
    span_width = rows * merge

    def normed_rows(side, begin, count):
        def one(index, carry):
            start = pl.multiple_of(begin + index * block, block)
            values = raw[side, pl.ds(start, block), :].astype(jnp.float32)
            mean_square = jnp.mean(values * values, axis=-1, keepdims=True)
            normed = values * lax.rsqrt(mean_square + epsilon) * gain_ref[...]
            target = pl.multiple_of(side * part_rows + start, block)
            for part in range(shards // merge):
                piece = normed[:, part * span_width : (part + 1) * span_width]
                split[part, pl.ds(target, block), :] = piece.astype(jnp.bfloat16)
            return carry

        lax.fori_loop(0, count // block, one, 0)

    normed_rows(group, 0, part_rows)
    key_sum[...] = jnp.zeros_like(key_sum)
    value_sum[...] = jnp.zeros_like(value_sum)
    query_sum[...] = jnp.zeros_like(query_sum)

    def products(total, columns, land, chip):
        if merge == 2:
            weights = land[pl.ds(chip * 2, 2), :, columns]
            weights = weights.reshape(2 * rows, weights.shape[-1])
            total[:, columns] += jnp.dot(
                split[chip], weights, preferred_element_type=jnp.float32
            )
        else:
            for side in range(2):
                total[:, columns] += jnp.dot(
                    split[chip * 2 + side],
                    land[chip * 2 + side, :, columns],
                    preferred_element_type=jnp.float32,
                )

    def key_value(step, carry):
        everything = pl.ds(0, width)
        products(key_sum, everything, key_land, ring.owner(1, step))
        products(value_sum, everything, value_land, ring.owner(-1, step))
        return carry

    def query(step, carry):
        products(query_sum, pl.ds(0, half), query_land, ring.owner(1, step))
        products(query_sum, pl.ds(half, half), query_land, ring.owner(-1, step))
        return carry

    def first_step(step, carry):
        ring.hop(first_flows, step)
        return carry

    lax.fori_loop(1, chips - 1, first_step, 0)
    ring.hop(second_flows, 0, first=True)
    ring.hop(first_flows, chips - 1, last=True)
    for piece in range(token_pieces - 1):
        token_copy(piece, 1 - group).wait_recv()
    normed_rows(1 - group, 0, part_rows - token_rows)

    def settle(step, carry):
        ring.landed(first_flows, step)
        return carry

    lax.fori_loop(0, chips, settle, 0)

    heads = width // HEAD_SIZE
    query_heads = query_ref.shape[1] // HEAD_SIZE

    def far_copy(index, own, target):
        return pltpu.make_async_remote_copy(
            src_ref=own,
            dst_ref=target.at[0],
            send_sem=far_send.at[index],
            recv_sem=far_recv.at[index],
            device_id=(far_to, group),
            device_id_type=MESH,
        )

    def near_copy(index, source, target):
        return pltpu.make_async_remote_copy(
            src_ref=source,
            dst_ref=target.at[1],
            send_sem=near_send.at[index],
            recv_sem=near_recv.at[index],
            device_id=(ring.other, group),
            device_id_type=MESH,
        )

    stacks = ((0, key_own, key_out), (1, value_own, value_out))

    def keep(index, own, target):
        return pltpu.make_async_copy(own, target.at[2], local_sem.at[index])

    def finish_keys():
        def one(head, carry):
            columns = pl.ds(pl.multiple_of(head * HEAD_SIZE, HEAD_SIZE), HEAD_SIZE)
            key_own[:, columns] = turned(
                key_sum[:, columns], key_gain_ref[...], cosine_ref[...], sine_ref[...], 1.0
            ).astype(jnp.bfloat16)
            return carry

        value_own[...] = value_sum[...].astype(jnp.bfloat16)
        lax.fori_loop(0, heads, one, 0)

    def send_keys():
        for index, own, target in stacks:
            keep(index, own, target).start()

            @pl.when(me + 2 < shards)
            def _():
                far_copy(index, own, target).start()

            @pl.when(core == 0)
            def _():
                near_copy(index, own, target).start()

    def second_step(step, carry):
        ring.hop(second_flows, step)
        ring.landed(second_flows, step - 1)

        @pl.when(step == 1)
        def _():
            token_copy(token_pieces - 1, 1 - group).wait_recv()
            normed_rows(1 - group, part_rows - token_rows, token_rows)
            lax.fori_loop(0, chips // 2, key_value, 0)

        @pl.when(step == 2)
        def _():
            lax.fori_loop(chips // 2, chips, key_value, 0)
            finish_keys()

        @pl.when(step == 3)
        def _():
            query(0, 0)
            send_keys()
            lax.fori_loop(1, 3, query, 0)

        @pl.when(step > 3)
        def _():
            query(step - 1, 0)

        return carry

    lax.fori_loop(1, chips - 1, second_step, 0)
    ring.hop(second_flows, chips - 1, last=True)
    ring.landed(second_flows, chips - 2)
    query(chips - 2, 0)

    @pl.when(me >= 2)
    def _():
        for index, own, target in stacks:
            far_copy(index, own, target).wait_recv()

            @pl.when(core == 1)
            def _():
                near_copy(index, target.at[0], target).start()

    ring.landed(second_flows, chips - 1)
    query(chips - 1, 0)

    def finish_query(head, carry):
        columns = pl.ds(pl.multiple_of(head * HEAD_SIZE, HEAD_SIZE), HEAD_SIZE)
        query_out[:, columns] = turned(
            query_sum[:, columns],
            query_gain_ref[...],
            cosine_ref[...],
            sine_ref[...],
            score_scale * log2_e,
        ).astype(jnp.bfloat16)
        return carry

    lax.fori_loop(0, query_heads, finish_query, 0)

    for index, own, target in stacks:
        keep(index, own, target).wait()

        @pl.when(me + 2 < shards)
        def _():
            far_copy(index, own, target).wait_send()

        @pl.when(core == 0)
        def _():
            near_copy(index, own, target).wait_send()

            @pl.when(me >= 2)
            def _():
                near_copy(index, own, target).wait_recv()

        @pl.when(core == 1)
        def _():
            near_copy(index, own, target).wait_recv()

            @pl.when(me >= 2)
            def _():
                near_copy(index, target.at[0], target).wait_send()

    for piece in range(token_pieces):
        token_copy(piece, group).wait_send()

    @pl.when(core != group)
    def _():
        swap.wait()

    ring.drain(first_flows)
    ring.drain(second_flows)


def attend_kernel(
    shards,
    query_ref,
    key_ref,
    value_ref,
    out_ref,
    swap_ref,
    tokens_ref,
    gain_ref,
    result_ref,
    out_land,
    key_window,
    value_window,
    attended,
    projected,
    gathered,
    ring_send,
    ring_recv,
    pair_send,
    pair_recv,
    load_sem,
    mixed_send,
    mixed_recv,
    back_send,
    back_recv,
):
    ring = Ring(shards, (ring_send, ring_recv, pair_send, pair_recv))
    chips, me, group, core = ring.chips, ring.me, ring.group, ring.core
    shard_rows = key_ref.shape[1]
    part_rows = tokens_ref.shape[0]
    heads = key_ref.shape[2] // HEAD_SIZE
    sharing = query_ref.shape[1] // key_ref.shape[2]
    head_width = sharing * HEAD_SIZE
    columns = query_ref.shape[1]
    half = columns // 2
    blocks = WINDOW_LENGTH // shard_rows + 1

    barrier = pltpu.get_barrier_semaphore()
    for device in (ring.other, ring.ahead, ring.behind):
        pl.semaphore_signal(barrier, inc=1, device_id=(device, group), device_id_type=MESH)
    pl.semaphore_signal(barrier, inc=1, device_id=(me, 1 - group), device_id_type=MESH)

    def own_copy(source):
        return pltpu.make_async_copy(
            source, out_land.at[me // 2, :, pl.ds(core * columns, columns)], load_sem.at[0]
        )

    @pl.when(core == group)
    def _():
        own_copy(out_ref).start()

    @pl.when(core != group)
    def _():
        own_copy(swap_ref).start()

    def window_copies(slot):
        span = pl.ds(slot * shard_rows, shard_rows)
        copies = [
            pltpu.make_async_copy(key_ref.at[slot], key_window.at[span], load_sem.at[1 + slot])
        ]
        for head in range(heads):
            copies.append(
                pltpu.make_async_copy(
                    value_ref.at[slot, :, pl.ds(head * HEAD_SIZE, HEAD_SIZE)],
                    value_window.at[head, span, pl.ds(0, HEAD_SIZE)],
                    load_sem.at[1 + blocks + slot * heads + head],
                )
            )
        return copies

    for slot in range(blocks):
        distance = blocks - 1 - slot
        span = pl.ds(slot * shard_rows, shard_rows)

        @pl.when(me >= distance)
        def _():
            for copy in window_copies(slot):
                copy.start()
            for head in range(heads):
                value_window[head, span, pl.ds(HEAD_SIZE, HEAD_SIZE)] = jnp.ones(
                    (shard_rows, HEAD_SIZE), jnp.bfloat16
                )

        @pl.when(me < distance)
        def _():
            key_window[span, :] = jnp.zeros((shard_rows, key_window.shape[1]), jnp.bfloat16)
            for head in range(heads):
                value_window[head, span, :] = jnp.zeros(
                    (shard_rows, 2 * HEAD_SIZE), jnp.bfloat16
                )

    pl.semaphore_wait(barrier, 4)

    wide = half // pieces

    def flow(index, column, way):
        def slot_of(chip, side):
            start = pl.multiple_of(side * columns + column, 128)
            return out_land.at[chip, :, pl.ds(start, wide)]

        return index, slot_of, way

    flows = []
    for piece in range(pieces):
        flows.append(flow(2 * piece, piece * wide, 1))
        flows.append(flow(2 * piece + 1, half + piece * wide, -1))

    own_copy(out_ref).wait()
    ring.hop(flows, 0, first=True)

    for slot in range(blocks):
        distance = blocks - 1 - slot

        @pl.when(me >= distance)
        def _():
            for copy in window_copies(slot):
                copy.wait()

    tile = part_rows
    tiles = shard_rows // tile
    reach = WINDOW_LENGTH // tile
    lower = lax.broadcasted_iota(jnp.int32, (tile, tile), 1) > lax.broadcasted_iota(
        jnp.int32, (tile, tile), 0
    )
    masks = jnp.concatenate([lower] * sharing, axis=0)

    def place_of(unit):
        head, part = unit // tiles, unit % tiles
        start = pl.multiple_of(part * tile, tile)
        column = pl.multiple_of(head * head_width, HEAD_SIZE)
        return head, start, column

    def attend(unit):
        head, start, column = place_of(unit)
        stacked = jnp.concatenate(
            [
                query_ref[
                    pl.ds(start, tile),
                    pl.ds(pl.multiple_of(column + i * HEAD_SIZE, HEAD_SIZE), HEAD_SIZE),
                ]
                for i in range(sharing)
            ],
            axis=0,
        )
        key_columns = pl.ds(pl.multiple_of(head * HEAD_SIZE, HEAD_SIZE), HEAD_SIZE)

        def scores(index):
            keys = key_window[pl.ds(start + index * tile, tile), key_columns]
            return lax.dot_general(
                stacked, keys, (((1,), (1,)), ((), ())), preferred_element_type=jnp.float32
            )

        def mixed(index, weights):
            values = value_window[head, pl.ds(start + index * tile, tile), :]
            return jnp.dot(
                weights.astype(jnp.bfloat16), values, preferred_element_type=jnp.float32
            )

        edge = jnp.exp2(jnp.where(masks, scores(0), scores(reach)))
        total = mixed(0, jnp.where(masks, edge, 0.0))
        total = total + mixed(reach, jnp.where(masks, 0.0, edge))
        for index in range(1, reach):
            total = total + mixed(index, jnp.exp2(scores(index)))
        final = (total[:, :HEAD_SIZE] / total[:, HEAD_SIZE:]).astype(jnp.bfloat16)
        for i in range(sharing):
            attended[
                group,
                pl.ds(start, tile),
                pl.ds(pl.multiple_of(column + i * HEAD_SIZE, HEAD_SIZE), HEAD_SIZE),
            ] = final[i * tile : (i + 1) * tile]

    def mixed_copy(unit, side):
        _, start, column = place_of(unit)
        piece = attended.at[side, pl.ds(start, tile), pl.ds(column, head_width)]
        return pltpu.make_async_remote_copy(
            src_ref=piece,
            dst_ref=piece,
            send_sem=mixed_send.at[unit],
            recv_sem=mixed_recv.at[unit],
            device_id=(me, 1 - group),
            device_id_type=MESH,
        )

    units = heads * tiles

    def attend_step(unit, carry):
        attend(unit)

        @pl.when(unit > 0)
        def _():
            mixed_copy(unit - 1, group).start()

        return carry

    lax.fori_loop(0, units // 2, attend_step, 0)
    ring.hop(flows, 1)
    lax.fori_loop(units // 2, units, attend_step, 0)
    ring.hop(flows, 2)
    mixed_copy(units - 1, group).start()
    ring.hop(flows, 3)

    def received(unit, carry):
        mixed_copy(unit, 1 - group).wait_recv()
        return carry

    lax.fori_loop(0, units, received, 0)

    def back_copy(chip, side):
        return pltpu.make_async_remote_copy(
            src_ref=projected.at[chip, pl.ds(pl.multiple_of((1 - group) * part_rows, 16), part_rows)],
            dst_ref=gathered.at[side, chip],
            send_sem=back_send.at[chip],
            recv_sem=back_recv.at[chip],
            device_id=(me, 1 - group),
            device_id_type=MESH,
        )

    def project(way, step):
        chip = ring.owner(way, step)
        weights = out_land.at[chip]
        total = lax.dot_general(
            attended[0],
            weights[:, :columns],
            (((1,), (1,)), ((), ())),
            preferred_element_type=jnp.float32,
        )
        total = total + lax.dot_general(
            attended[1],
            weights[:, columns:],
            (((1,), (1,)), ((), ())),
            preferred_element_type=jnp.float32,
        )
        projected[chip] = total.astype(jnp.bfloat16)
        gathered[group, chip] = projected[
            chip, pl.ds(pl.multiple_of(group * part_rows, 16), part_rows)
        ]
        back_copy(chip, group).start()

    def landed(way, step):
        ring.landed([f for f in flows if f[2] == way], step)

    landed(1, 0)
    landed(-1, 0)
    project(1, 0)
    middle = chips // 2

    def early(step, carry):
        landed(1, step)
        landed(-1, step)
        return carry

    lax.fori_loop(1, 4, early, 0)

    def later(step, carry):
        ring.hop(flows, step)
        landed(1, step)
        landed(-1, step)

        @pl.when(step >= middle)
        def _():
            project(1, step)

            @pl.when(step > middle)
            def _():
                project(-1, step)

        return carry

    lax.fori_loop(4, chips - 1, later, 0)
    ring.hop(flows, chips - 1, last=True)
    landed(1, chips - 1)
    landed(-1, chips - 1)
    project(1, chips - 1)
    project(-1, chips - 1)

    def arrived(chip, carry):
        back_copy(chip, 1 - group).wait_recv()
        return carry

    lax.fori_loop(0, chips, arrived, 0)

    block = 16

    def final(index, carry):
        start = pl.multiple_of(index * block, block)
        values = jnp.concatenate(
            [
                gathered[side, chip, pl.ds(start, block), :].astype(jnp.float32)
                for chip in range(chips)
                for side in range(2)
            ],
            axis=1,
        )
        mean_square = jnp.mean(values * values, axis=-1, keepdims=True)
        scaled = values * lax.rsqrt(mean_square + epsilon) * gain_ref[...]
        rows = tokens_ref[pl.ds(start, block), :].astype(jnp.float32)
        result_ref[pl.ds(start, block), :] = (rows + scaled).astype(jnp.bfloat16)
        return carry

    lax.fori_loop(0, part_rows // block, final, 0)

    def sent(unit, carry):
        mixed_copy(unit, group).wait_send()
        return carry

    lax.fori_loop(0, units, sent, 0)

    def back_sent(chip, carry):
        back_copy(chip, group).wait_send()
        return carry

    lax.fori_loop(0, chips, back_sent, 0)
    ring.drain(flows)


def ring_semaphores(flows, chips):
    return [pltpu.SemaphoreType.DMA((flows, chips))] * 4


def on_device(
    tokens,
    norm_gain,
    query_weight,
    key_matrix,
    value_matrix,
    out_weight,
    query_gain,
    key_gain,
    post_gain,
):
    shards = lax.axis_size("seq")
    copies = lax.axis_size("fsdp")
    chips = shards // 2
    part_rows, model_width = tokens.shape
    shard_rows = part_rows * copies
    rows, query_width = query_weight.shape
    key_width = key_matrix.shape[1]
    merge = 2 if rows % 16 == 0 else 1
    blocks = WINDOW_LENGTH // shard_rows + 1

    positions = lax.axis_index("seq") * shard_rows + jnp.arange(shard_rows, dtype=jnp.int32)
    exponents = jnp.arange(HEAD_SIZE // 2, dtype=jnp.float32) * (2.0 / HEAD_SIZE)
    frequency = jnp.exp(-exponents * jnp.log(jnp.float32(rope_base)))
    angles = positions.astype(jnp.float32)[:, None] * frequency[None, :]
    cosine, sine = jnp.cos(angles), jnp.sin(angles)
    cosine = jnp.concatenate([cosine, cosine], axis=1)
    sine = jnp.concatenate([-sine, sine], axis=1)

    hbm = pl.BlockSpec(memory_space=pltpu.MemorySpace.HBM)
    vmem = pl.BlockSpec(memory_space=pltpu.VMEM)
    bf16, f32 = jnp.bfloat16, jnp.float32
    dma = pltpu.SemaphoreType.DMA
    stack = jax.ShapeDtypeStruct((blocks, shard_rows, key_width), bf16)
    queries, keys, values, swapped = pl.pallas_call(
        functools.partial(project_kernel, shards, merge),
        out_shape=[
            jax.ShapeDtypeStruct((shard_rows, query_width), bf16),
            stack,
            stack,
            jax.ShapeDtypeStruct(out_weight.shape, bf16),
        ],
        in_specs=[hbm, vmem, hbm, hbm, hbm, hbm, vmem, vmem, vmem, vmem],
        out_specs=[vmem, hbm, hbm, hbm],
        scratch_shapes=[
            pltpu.VMEM((shards, rows, query_width), bf16),
            pltpu.VMEM((shards, rows, key_width), bf16),
            pltpu.VMEM((shards, rows, key_width), bf16),
            pltpu.VMEM((copies, part_rows, model_width), bf16),
            pltpu.VMEM((shards // merge, shard_rows, merge * rows), bf16),
            pltpu.VMEM((shard_rows, query_width), f32),
            pltpu.VMEM((shard_rows, key_width), f32),
            pltpu.VMEM((shard_rows, key_width), f32),
            pltpu.VMEM((shard_rows, key_width), bf16),
            pltpu.VMEM((shard_rows, key_width), bf16),
            *ring_semaphores(4 * pieces, chips),
            dma((4,)),
            dma((token_pieces,)),
            dma((token_pieces,)),
            dma((2,)),
            dma((2,)),
            dma((2,)),
            dma((2,)),
            dma((2,)),
        ],
        compiler_params=pltpu.CompilerParams(
            collective_id=0, has_side_effects=True, vmem_limit_bytes=60 * 1024 * 1024
        ),
    )(
        tokens,
        norm_gain[None, :],
        query_weight,
        key_matrix,
        value_matrix,
        out_weight,
        query_gain[None, :],
        key_gain[None, :],
        cosine,
        sine,
    )
    heads = key_width // HEAD_SIZE
    units = heads * copies
    window = blocks * shard_rows
    return pl.pallas_call(
        functools.partial(attend_kernel, shards),
        out_shape=jax.ShapeDtypeStruct(tokens.shape, bf16),
        in_specs=[vmem, hbm, hbm, hbm, hbm, vmem, vmem],
        out_specs=vmem,
        scratch_shapes=[
            pltpu.VMEM((chips, rows, 2 * query_width), bf16),
            pltpu.VMEM((window, key_width), bf16),
            pltpu.VMEM((heads, window, 2 * HEAD_SIZE), bf16),
            pltpu.VMEM((copies, shard_rows, query_width), bf16),
            pltpu.VMEM((chips, shard_rows, rows), bf16),
            pltpu.VMEM((copies, chips, part_rows, rows), bf16),
            *ring_semaphores(2 * pieces, chips),
            dma((1 + blocks * (1 + heads),)),
            dma((units,)),
            dma((units,)),
            dma((chips,)),
            dma((chips,)),
        ],
        compiler_params=pltpu.CompilerParams(
            collective_id=1, has_side_effects=True, vmem_limit_bytes=60 * 1024 * 1024
        ),
    )(queries, keys, values, out_weight, swapped, tokens, post_gain[None, :])


def solution(mesh):
    in_specs = (
        P(("seq", "fsdp"), None),
        P(),
        P("seq", "fsdp"),
        P("seq", "fsdp"),
        P("seq", "fsdp"),
        P("seq", "fsdp"),
        P(),
        P(),
        P(),
    )
    out_specs = P(("seq", "fsdp"), None)
    return jax.shard_map(
        on_device, mesh=mesh, in_specs=in_specs, out_specs=out_specs, check_vma=False
    )
```

time: 349 us -> 231 us (0.66); the launches traced: 342 us -> 228 us
  Pallas kernels: 129 us -> 220 us
  waiting for transfers between devices: 72.3 us -> 0 us
  matrix products: 63.9 us -> 0 us
  local copies, waits for them, and re-layouts: 35.4 us -> 6.21 us
  other arithmetic: 18.9 us -> 1.98 us
  between operations: 14.2 us -> 0.03 us
  starting transfers between devices: 8.24 us -> 0 us
    pallas_call x1 -> x2, Pallas kernels: 129 us -> 220 us  [the longest x1 140 us: on_device(): pl.pallas_call(functools.partial(project_kernel, shards, merge), out_shap...]
    ppermute x3 -> x0, waiting for transfers between devices: 72.3 us -> none  [the longest x1 42 us: on_device(): summed = summed + lax.ppermute(away, 'fsdp', route).astype(jnp.float32)]
    dot_general x7 -> x0, matrix products: 54.1 us -> none  [the longest x2 17.4 us: partial_rows(): lax.dot_general(attended, out_full, (((1,), (1,)), ((), ())), preferred_e...]
    dot_general x2 -> x0, local copies, waits for them, and re-layouts: 22.5 us -> none  [the longest x1 14.2 us: on_device(): jnp.dot(normed_input, query_full, preferred_element_type=jnp.float32)]
    sub x2 -> x0, matrix products: 9.79 us -> none  [window_block(): raised = jnp.exp(scores - highest)]
    ppermute x3 -> x0, starting transfers between devices: 8.24 us -> none  [the longest x2 7.09 us: passed_along(): return lax.ppermute(block, axis, route)]
    another operation x4 -> x0, local copies, waits for them, and re-layouts: 8.23 us -> none  [the longest x2 4.34 us: partial_rows(): keys = window[0].reshape(part_keys, local_heads, HEAD_SIZE)]
    convert_element_type x2 -> x1, other arithmetic: 4.54 us -> 0.01 us  [on_device(): angles = positions.astype(jnp.float32)[:, None] * frequency[None, :]]
  transfers between devices with their start and end apart: 4 -> 0, of which waited for: 2 -> 0; matrix products, arithmetic and copies ran while one was open for 28% -> 0% of each run, Pallas kernels for 0% -> 0%
where the time goes in v1:
time: 231 us; the launch traced here: 228 us
  Pallas kernels  220 us (95%)
  local copies, waits for them, and re-layouts  6.21 us (3%)
    pallas_call x1, Pallas kernels, on_device(): pl.pallas_call(functools.partial(project_kernel, shards, merge), out_shap...  140 us
    pallas_call x1, Pallas kernels, on_device(): pl.pallas_call(functools.partial(attend_kernel, shards), out_shape=jax.Sh...  79.3 us

profile of v1, /device:TPU:5, one launch (start us, length us, event | category | flops | bytes accessed | tf_op | source)
XLA Modules:
  0.0 227.8 jit_solution(14112673452257758320)
XLA Ops:
  0.0 1.4 broadcast_in_dim.14.gain_ref
  1.4 1.4 broadcast_in_dim.17.gain_ref
  2.7 1.0 fusion
  3.7 1.0 pad_maximum_fusion
  4.7 140.3 %shard_map.91 = (bf16[512,1024]{1,0:T(8,128)(2,1)}, bf16[3,512,512]{2,1,0:T(8,128)(2,1)}, bf16[3,512,512]{2,1,0:T(8,128)(2,1)}, bf16[336,1024]{1,0:T(8,128)(2,1)}) custom-call(bf16[256,5376]{1,0:T(8,128)(2,1)} %tokens_ref.3, f32[1,5376]{1,0:T(1,128)} %broadcast_in_dim.14.gain_ref, bf16[336,1024]{1,0:T(8,128)(2,1)} %query_ref.1, bf16[336,512]{1,0:T(8,128)(2,1)} %key_ref.1, ...), custom_call_target="tpu_custom_call" | custom-call | tf_op jit(solution)/shard_map/pallas_call | solution.py:798
  145.1 79.3 %shard_map.92 = bf16[256,5376]{1,0:T(8,128)(2,1)} custom-call(bf16[512,1024]{1,0:T(8,128)(2,1)} %get-tuple-element.9.query_ref, bf16[3,512,512]{2,1,0:T(8,128)(2,1)} %get-tuple-element.10.key_ref, bf16[3,512,512]{2,1,0:T(8,128)(2,1)} %get-tuple-element.11.value_ref, bf16[336,1024]{1,0:T(8,128)(2,1)} %out_ref.3, ...), custom_call_target="tpu_custom_call" | custom-call | tf_op jit(solution)/shard_map/pallas_call | solution.py:847
  224.3 3.5 %copy.11 = bf16[256,5376]{1,0:T(8,128)(2,1)} copy(bf16[256,5376]{1,0:T(8,128)(2,1)} %shard_map.92) | data formatting | bytes 5505024
  (2 shorter events, 0.0 us)

commit v2 on v1

v2 whole, which is shorter than its diff:
```python
import functools

import jax
import jax.numpy as jnp
from jax import lax
from jax.experimental import pallas as pl
from jax.experimental.pallas import tpu as pltpu
from jax.sharding import PartitionSpec as P

HEAD_SIZE = 128
WINDOW_LENGTH = 1024

epsilon = 1e-06
score_scale = 168.0 ** (-0.5)
log2_e = 1.4426950408889634
rope_base = 10000.0
pieces = 2
token_pieces = 4
MESH = pl.DeviceIdType.MESH


def ring_place(chip, chips):
    row, side = chip // 2, chip % 2
    return side * (chips - 1 - row) + (1 - side) * row


def ring_chip(place, chips):
    back = place // (chips // 2)
    return back * (2 * (chips - 1 - place) + 1) + (1 - back) * 2 * place


class Ring:
    def __init__(self, shards, sems):
        self.chips = shards // 2
        self.me = lax.axis_index("seq")
        self.group = lax.axis_index("fsdp")
        self.core = self.me % 2
        self.place = ring_place(self.me // 2, self.chips)
        self.other = (self.me // 2) * 2 + 1 - self.core
        self.ahead = self.neighbour(1)
        self.behind = self.neighbour(self.chips - 1)
        self.ring_send, self.ring_recv, self.pair_send, self.pair_recv = sems

    def neighbour(self, distance):
        return ring_chip((self.place + distance) % self.chips, self.chips) * 2 + self.core

    def owner(self, way, step):
        return ring_chip((self.place + (self.chips - way) * step) % self.chips, self.chips)

    def ring_copy(self, flow, step, sent):
        index, slot_of, way = flow
        slot = slot_of(self.owner(way, step), self.core)
        return pltpu.make_async_remote_copy(
            src_ref=slot,
            dst_ref=slot,
            send_sem=self.ring_send.at[index, sent],
            recv_sem=self.ring_recv.at[index, sent],
            device_id=(self.ahead if way > 0 else self.behind, self.group),
            device_id_type=MESH,
        )

    def pair_copy(self, flow, step, core):
        index, slot_of, way = flow
        slot = slot_of(self.owner(way, step), core)
        return pltpu.make_async_remote_copy(
            src_ref=slot,
            dst_ref=slot,
            send_sem=self.pair_send.at[index, step],
            recv_sem=self.pair_recv.at[index, step],
            device_id=(self.other, self.group),
            device_id_type=MESH,
        )

    def hop(self, step, flows, arrive=None, leave=None, hand=None):
        for flow in flows:
            if arrive is None or flow in arrive:
                self.ring_copy(flow, step, step - 1).wait_recv()
            if leave is None or flow in leave:
                self.ring_copy(flow, step, step).start()
            if hand is None or flow in hand:
                self.pair_copy(flow, step, self.core).start()

    def landed(self, flows, step):
        for flow in flows:
            self.pair_copy(flow, step, 1 - self.core).wait_recv()

    def sent(self, step, leave, hand):
        for flow in leave:
            self.ring_copy(flow, step, step).wait_send()
        for flow in hand:
            self.pair_copy(flow, step, self.core).wait_send()


def steps(first, last, body):
    def one(step, carry):
        body(step)
        return carry

    lax.fori_loop(first, last, one, 0)


def turned(values, gain, cosine, sine, scale):
    mean_square = jnp.mean(values * values, axis=-1, keepdims=True)
    normed = values * lax.rsqrt(mean_square + epsilon) * gain
    swapped = pltpu.roll(normed, values.shape[-1] // 2, 1)
    return (normed * cosine + swapped * sine) * scale


def layer_kernel(
    shards,
    merge,
    tokens_ref,
    gain_ref,
    query_ref,
    key_ref,
    value_ref,
    out_ref,
    query_gain_ref,
    key_gain_ref,
    post_gain_ref,
    cosine_ref,
    sine_ref,
    result_ref,
    swap_out,
    query_land,
    pair_land,
    raw,
    split,
    query_sum,
    key_sum,
    value_sum,
    queries,
    key_window,
    value_window,
    attended,
    projected,
    gathered,
    cosines,
    sines,
    ring_send,
    ring_recv,
    pair_send,
    pair_recv,
    local_sem,
    token_send,
    token_recv,
    swap_sem,
    far_send,
    far_recv,
    near_send,
    near_recv,
    mixed_send,
    mixed_recv,
    back_send,
    back_recv,
    free_sem,
):
    ring = Ring(shards, (ring_send, ring_recv, pair_send, pair_recv))
    chips, me, group, core = ring.chips, ring.me, ring.group, ring.core
    rows, width = key_ref.shape
    part_rows = tokens_ref.shape[0]
    columns = query_ref.shape[1]
    half = columns // 2
    shard_rows = queries.shape[0]
    heads = width // HEAD_SIZE
    query_heads = columns // HEAD_SIZE
    sharing = query_heads // heads
    head_width = sharing * HEAD_SIZE
    blocks = WINDOW_LENGTH // shard_rows + 1
    far_to = (me + 2) % shards
    far_from = (me + shards - 2) % shards
    middle = chips // 2

    barrier = pltpu.get_barrier_semaphore()
    for device in (ring.other, ring.ahead, ring.behind, far_to, far_from):
        pl.semaphore_signal(barrier, inc=1, device_id=(device, group), device_id_type=MESH)
    pl.semaphore_signal(barrier, inc=1, device_id=(me, 1 - group), device_id_type=MESH)

    @pl.when(core != group)
    def _():
        pl.semaphore_signal(
            barrier,
            inc=1,
            device_id=((me // 2) * 2 + group, core),
            device_id_type=MESH,
        )

    local = [
        pltpu.make_async_copy(key_ref, pair_land.at[me, :, pl.ds(0, width)], local_sem.at[0]),
        pltpu.make_async_copy(
            value_ref, pair_land.at[me, :, pl.ds(width, width)], local_sem.at[1]
        ),
        pltpu.make_async_copy(query_ref, query_land.at[me], local_sem.at[2]),
        pltpu.make_async_copy(tokens_ref, raw.at[group], local_sem.at[3]),
    ]
    for copy in local:
        copy.start()
    pl.semaphore_wait(barrier, 6 + (core + group) % 2)

    def flow(index, land, column, count, way):
        return index, lambda chip, side: land.at[chip * 2 + side, :, pl.ds(column, count)], way

    size, wide = width // pieces, half // pieces
    first, second = [], []
    for piece in range(pieces):
        first.append(flow(2 * piece, pair_land, piece * size, size, 1))
        first.append(flow(2 * piece + 1, pair_land, width + piece * size, size, -1))
    for piece in range(pieces):
        base = 2 * (pieces + piece)
        second.append(flow(base, query_land, piece * wide, wide, 1))
        second.append(flow(base + 1, query_land, half + piece * wide, wide, -1))
    third = []
    for piece in range(2):
        for way in (1, -1):
            third.append(flow(4 * pieces + len(third), pair_land, piece * half, half, way))
    origin = [third[0], third[2]]
    farthest = [third[0], third[3]]

    token_rows = part_rows // token_pieces

    def token_copy(piece, side):
        span = pl.ds(piece * token_rows, token_rows)
        return pltpu.make_async_remote_copy(
            src_ref=tokens_ref.at[span],
            dst_ref=raw.at[side, span],
            send_sem=token_send.at[piece],
            recv_sem=token_recv.at[piece],
            device_id=(me, 1 - group),
            device_id_type=MESH,
        )

    swap = pltpu.make_async_remote_copy(
        src_ref=out_ref,
        dst_ref=swap_out,
        send_sem=swap_sem.at[0],
        recv_sem=swap_sem.at[1],
        device_id=((me // 2) * 2 + group, core),
        device_id_type=MESH,
    )

    local[0].wait()
    local[1].wait()
    ring.hop(0, first, arrive=[])
    for piece in range(token_pieces):
        token_copy(piece, group).start()

    @pl.when(core != group)
    def _():
        swap.start()

    local[2].wait()
    local[3].wait()

    block = 16
    span_width = rows * merge

    def normed_rows(side, begin, count):
        def one(index):
            start = pl.multiple_of(begin + index * block, block)
            values = raw[side, pl.ds(start, block), :].astype(jnp.float32)
            mean_square = jnp.mean(values * values, axis=-1, keepdims=True)
            normed = values * lax.rsqrt(mean_square + epsilon) * gain_ref[...][None, :]
            target = pl.multiple_of(side * part_rows + start, block)
            for part in range(shards // merge):
                piece = normed[:, part * span_width : (part + 1) * span_width]
                split[part, pl.ds(target, block), :] = piece.astype(jnp.bfloat16)

        steps(0, count // block, one)

    normed_rows(group, 0, part_rows)
    key_sum[...] = jnp.zeros_like(key_sum)
    value_sum[...] = jnp.zeros_like(value_sum)
    query_sum[...] = jnp.zeros_like(query_sum)
    cosines[...] = jnp.concatenate([cosine_ref[...], cosine_ref[...]], axis=1)
    sines[...] = jnp.concatenate([-sine_ref[...], sine_ref[...]], axis=1)

    for slot in range(blocks - 1):
        distance = blocks - 1 - slot
        span = pl.ds(slot * shard_rows, shard_rows)

        @pl.when(me < distance)
        def _():
            key_window[span, :] = jnp.zeros((shard_rows, width), jnp.bfloat16)
            for head in range(heads):
                value_window[head, span, :] = jnp.zeros(
                    (shard_rows, 2 * HEAD_SIZE), jnp.bfloat16
                )

    for slot in range(blocks):
        span = pl.ds(slot * shard_rows, shard_rows)

        @pl.when(me >= blocks - 1 - slot)
        def _():
            for head in range(heads):
                value_window[head, span, pl.ds(HEAD_SIZE, HEAD_SIZE)] = jnp.ones(
                    (shard_rows, HEAD_SIZE), jnp.bfloat16
                )

    def products(total, begin, land, column, count, chip):
        target = pl.ds(begin, count)
        taken = pl.ds(column, count)
        if merge == 2:
            weights = land[pl.ds(chip * 2, 2), :, taken].reshape(2 * rows, count)
            total[:, target] += jnp.dot(
                split[chip], weights, preferred_element_type=jnp.float32
            )
        else:
            for side in range(2):
                total[:, target] += jnp.dot(
                    split[chip * 2 + side],
                    land[chip * 2 + side, :, taken],
                    preferred_element_type=jnp.float32,
                )

    def key_value(step):
        products(key_sum, 0, pair_land, 0, width, ring.owner(1, step))
        products(value_sum, 0, pair_land, width, width, ring.owner(-1, step))

    def query(step):
        products(query_sum, 0, query_land, 0, half, ring.owner(1, step))
        products(query_sum, half, query_land, half, half, ring.owner(-1, step))

    steps(1, chips - 1, lambda step: ring.hop(step, first))
    ring.hop(0, second, arrive=[])
    ring.hop(chips - 1, first, leave=[])
    for piece in range(token_pieces - 1):
        token_copy(piece, 1 - group).wait_recv()
    normed_rows(1 - group, 0, part_rows - token_rows)
    steps(0, chips, lambda step: ring.landed(first, step))

    def span_of(slot):
        return pl.ds(slot * shard_rows, shard_rows)

    def key_part(slot):
        return key_window.at[span_of(slot)]

    def value_part(slot):
        return value_window.at[:, span_of(slot), pl.ds(0, HEAD_SIZE)]

    stacks = ((0, key_part), (1, value_part))

    def far_copy(index, part):
        return pltpu.make_async_remote_copy(
            src_ref=part(blocks - 1),
            dst_ref=part(0),
            send_sem=far_send.at[index],
            recv_sem=far_recv.at[index],
            device_id=(far_to, group),
            device_id_type=MESH,
        )

    def near_copy(index, part, slot):
        return pltpu.make_async_remote_copy(
            src_ref=part(slot),
            dst_ref=part(1),
            send_sem=near_send.at[index],
            recv_sem=near_recv.at[index],
            device_id=(ring.other, group),
            device_id_type=MESH,
        )

    def head_columns(head):
        return pl.ds(pl.multiple_of(head * HEAD_SIZE, HEAD_SIZE), HEAD_SIZE)

    def finish_keys():
        def one(head):
            taken = head_columns(head)
            key_window[span_of(blocks - 1), taken] = turned(
                key_sum[:, taken], key_gain_ref[...][None, :], cosines[...], sines[...], 1.0
            ).astype(jnp.bfloat16)
            value_window[head, span_of(blocks - 1), pl.ds(0, HEAD_SIZE)] = value_sum[
                :, taken
            ].astype(jnp.bfloat16)

        steps(0, heads, one)

    def send_keys():
        for index, part in stacks:

            @pl.when(me + 2 < shards)
            def _():
                far_copy(index, part).start()

            @pl.when(core == 0)
            def _():
                near_copy(index, part, blocks - 1).start()

    def own_copy(source):
        return pltpu.make_async_copy(source, pair_land.at[me], local_sem.at[0])

    def free_slots():
        steps(0, chips - 1, lambda step: ring.sent(step, first, first))
        ring.sent(chips - 1, [], first)
        for device in (ring.other, ring.ahead, ring.behind):
            pl.semaphore_signal(
                free_sem, inc=1, device_id=(device, group), device_id_type=MESH
            )

        @pl.when(core == group)
        def _():
            own_copy(out_ref).start()

        @pl.when(core != group)
        def _():
            swap.wait()
            own_copy(swap_out).start()

    def second_step(step):
        ring.hop(step, second)
        ring.landed(second, step - 1)

        @pl.when(step == 1)
        def _():
            token_copy(token_pieces - 1, 1 - group).wait_recv()
            normed_rows(1 - group, part_rows - token_rows, token_rows)
            steps(0, middle, key_value)

        @pl.when(step == 2)
        def _():
            steps(middle, chips, key_value)
            finish_keys()

        @pl.when(step == 3)
        def _():
            query(0)
            send_keys()
            steps(1, 3, query)

        @pl.when(step > 3)
        def _():
            query(step - 1)

        @pl.when(step == 4)
        def _():
            free_slots()

    steps(1, chips - 1, second_step)

    pl.semaphore_wait(free_sem, 3)
    own_copy(out_ref).wait()
    ring.hop(0, third, arrive=[], hand=origin)
    ring.hop(chips - 1, second, leave=[])
    ring.landed(second, chips - 2)
    query(chips - 2)

    @pl.when(me >= 2)
    def _():
        for index, part in stacks:
            far_copy(index, part).wait_recv()

            @pl.when(core == 1)
            def _():
                near_copy(index, part, 0).start()

    ring.landed(second, chips - 1)
    query(chips - 1)

    def finish_query(head):
        taken = head_columns(head)
        queries[:, taken] = turned(
            query_sum[:, taken],
            query_gain_ref[...][None, :],
            cosines[...],
            sines[...],
            score_scale * log2_e,
        ).astype(jnp.bfloat16)

    steps(0, query_heads, finish_query)

    for index, part in stacks:

        @pl.when(core == 1)
        def _():
            near_copy(index, part, 0).wait_recv()

        @pl.when(core == 0)
        def _():
            @pl.when(me >= 2)
            def _():
                near_copy(index, part, 0).wait_recv()

    tile = part_rows
    tiles = shard_rows // tile
    reach = WINDOW_LENGTH // tile
    lower = lax.broadcasted_iota(jnp.int32, (tile, tile), 1) > lax.broadcasted_iota(
        jnp.int32, (tile, tile), 0
    )
    masks = jnp.concatenate([lower] * sharing, axis=0)

    def place_of(unit):
        head, part = unit // tiles, unit % tiles
        start = pl.multiple_of(part * tile, tile)
        column = pl.multiple_of(head * head_width, HEAD_SIZE)
        return head, start, column

    def attend(unit):
        head, start, column = place_of(unit)
        taken = [
            pl.ds(pl.multiple_of(column + i * HEAD_SIZE, HEAD_SIZE), HEAD_SIZE)
            for i in range(sharing)
        ]
        stacked = jnp.concatenate([queries[pl.ds(start, tile), c] for c in taken], axis=0)
        key_columns = head_columns(head)

        def scores(index):
            keys = key_window[pl.ds(start + index * tile, tile), key_columns]
            return lax.dot_general(
                stacked, keys, (((1,), (1,)), ((), ())), preferred_element_type=jnp.float32
            )

        def mixed(index, weights):
            values = value_window[head, pl.ds(start + index * tile, tile), :]
            return jnp.dot(
                weights.astype(jnp.bfloat16), values, preferred_element_type=jnp.float32
            )

        edge = jnp.exp2(jnp.where(masks, scores(0), scores(reach)))
        total = mixed(0, jnp.where(masks, edge, 0.0))
        total = total + mixed(reach, jnp.where(masks, 0.0, edge))
        for index in range(1, reach):
            total = total + mixed(index, jnp.exp2(scores(index)))
        final = (total[:, :HEAD_SIZE] / total[:, HEAD_SIZE:]).astype(jnp.bfloat16)
        for i in range(sharing):
            attended[group, pl.ds(start, tile), taken[i]] = final[i * tile : (i + 1) * tile]

    def mixed_copy(unit, side):
        _, start, column = place_of(unit)
        piece = attended.at[side, pl.ds(start, tile), pl.ds(column, head_width)]
        return pltpu.make_async_remote_copy(
            src_ref=piece,
            dst_ref=piece,
            send_sem=mixed_send.at[unit],
            recv_sem=mixed_recv.at[unit],
            device_id=(me, 1 - group),
            device_id_type=MESH,
        )

    units = heads * tiles

    def attend_step(unit):
        attend(unit)

        @pl.when(unit > 0)
        def _():
            mixed_copy(unit - 1, group).start()

    def back_copy(chip, side):
        away = pl.multiple_of((1 - group) * part_rows, 16)
        return pltpu.make_async_remote_copy(
            src_ref=projected.at[chip, pl.ds(away, part_rows)],
            dst_ref=gathered.at[side, chip],
            send_sem=back_send.at[chip],
            recv_sem=back_recv.at[chip],
            device_id=(me, 1 - group),
            device_id_type=MESH,
        )

    def project(way, step):
        chip = ring.owner(way, step)
        parts = [
            lax.dot_general(
                attended[side],
                pair_land[chip * 2 + side],
                (((1,), (1,)), ((), ())),
                preferred_element_type=jnp.float32,
            )
            for side in range(2)
        ]
        projected[chip] = (parts[0] + parts[1]).astype(jnp.bfloat16)
        home = pl.multiple_of(group * part_rows, 16)
        gathered[group, chip] = projected[chip, pl.ds(home, part_rows)]
        back_copy(chip, group).start()

    steps(0, units, attend_step)
    ring.hop(1, third)
    mixed_copy(units - 1, group).start()
    steps(0, units, lambda unit: mixed_copy(unit, 1 - group).wait_recv())
    ring.landed(origin, 0)
    project(1, 0)

    def both(step):
        ring.landed(third, step)
        project(1, step)
        project(-1, step)

    def third_step(step):
        both(step - 1)
        ring.hop(step, third)

    steps(2, middle - 1, third_step)
    both(middle - 2)
    ring.hop(middle - 1, third, leave=farthest)
    both(middle - 1)
    ring.hop(middle, farthest, leave=[])
    ring.landed(farthest, middle)
    project(1, middle)
    steps(0, chips, lambda chip: back_copy(chip, 1 - group).wait_recv())

    def final(index):
        start = pl.multiple_of(index * block, block)
        values = jnp.concatenate(
            [
                gathered[side, chip, pl.ds(start, block), :].astype(jnp.float32)
                for chip in range(chips)
                for side in range(2)
            ],
            axis=1,
        )
        mean_square = jnp.mean(values * values, axis=-1, keepdims=True)
        scaled = values * lax.rsqrt(mean_square + epsilon) * post_gain_ref[...][None, :]
        added = raw[group, pl.ds(start, block), :].astype(jnp.float32) + scaled
        result_ref[pl.ds(start, block), :] = added.astype(jnp.bfloat16)

    steps(0, part_rows // block, final)

    for index, part in stacks:

        @pl.when(me + 2 < shards)
        def _():
            far_copy(index, part).wait_send()

        @pl.when(core == 0)
        def _():
            near_copy(index, part, blocks - 1).wait_send()

        @pl.when(core == 1)
        def _():
            @pl.when(me >= 2)
            def _():
                near_copy(index, part, 0).wait_send()

    for piece in range(token_pieces):
        token_copy(piece, group).wait_send()
    steps(0, chips - 1, lambda step: ring.sent(step, second, second))
    ring.sent(chips - 1, [], second)
    ring.sent(0, third, origin)
    steps(1, middle - 1, lambda step: ring.sent(step, third, third))
    ring.sent(middle - 1, farthest, third)
    ring.sent(middle, [], farthest)
    steps(0, units, lambda unit: mixed_copy(unit, group).wait_send())
    steps(0, chips, lambda chip: back_copy(chip, group).wait_send())


def on_device(
    tokens,
    norm_gain,
    query_weight,
    key_matrix,
    value_matrix,
    out_weight,
    query_gain,
    key_gain,
    post_gain,
):
    shards = lax.axis_size("seq")
    copies = lax.axis_size("fsdp")
    chips = shards // 2
    part_rows, model_width = tokens.shape
    shard_rows = part_rows * copies
    rows, query_width = query_weight.shape
    key_width = key_matrix.shape[1]
    merge = 2 if rows % 16 == 0 else 1
    heads = key_width // HEAD_SIZE
    units = heads * copies
    window = WINDOW_LENGTH + shard_rows

    positions = lax.axis_index("seq") * shard_rows + jnp.arange(shard_rows, dtype=jnp.int32)
    exponents = jnp.arange(HEAD_SIZE // 2, dtype=jnp.float32) * (2.0 / HEAD_SIZE)
    frequency = jnp.exp(-exponents * jnp.log(jnp.float32(rope_base)))
    angles = positions.astype(jnp.float32)[:, None] * frequency[None, :]

    hbm = pl.BlockSpec(memory_space=pltpu.MemorySpace.HBM)
    vmem = pl.BlockSpec(memory_space=pltpu.VMEM)
    bf16, f32 = jnp.bfloat16, jnp.float32
    dma = pltpu.SemaphoreType.DMA
    result, _ = pl.pallas_call(
        functools.partial(layer_kernel, shards, merge),
        out_shape=[
            jax.ShapeDtypeStruct(tokens.shape, bf16),
            jax.ShapeDtypeStruct(out_weight.shape, bf16),
        ],
        in_specs=[hbm, vmem, hbm, hbm, hbm, hbm, vmem, vmem, vmem, vmem, vmem],
        out_specs=[vmem, hbm],
        scratch_shapes=[
            pltpu.VMEM((shards, rows, query_width), bf16),
            pltpu.VMEM((shards, rows, query_width), bf16),
            pltpu.VMEM((copies, part_rows, model_width), bf16),
            pltpu.VMEM((shards // merge, shard_rows, merge * rows), bf16),
            pltpu.VMEM((shard_rows, query_width), f32),
            pltpu.VMEM((shard_rows, key_width), f32),
            pltpu.VMEM((shard_rows, key_width), f32),
            pltpu.VMEM((shard_rows, query_width), bf16),
            pltpu.VMEM((window, key_width), bf16),
            pltpu.VMEM((heads, window, 2 * HEAD_SIZE), bf16),
            pltpu.VMEM((copies, shard_rows, query_width), bf16),
            pltpu.VMEM((chips, shard_rows, rows), bf16),
            pltpu.VMEM((copies, chips, part_rows, rows), bf16),
            pltpu.VMEM((shard_rows, HEAD_SIZE), f32),
            pltpu.VMEM((shard_rows, HEAD_SIZE), f32),
            *[dma((4 * pieces + 4, chips))] * 4,
            dma((4,)),
            dma((token_pieces,)),
            dma((token_pieces,)),
            dma((2,)),
            dma((2,)),
            dma((2,)),
            dma((2,)),
            dma((2,)),
            dma((units,)),
            dma((units,)),
            dma((chips,)),
            dma((chips,)),
            pltpu.SemaphoreType.REGULAR,
        ],
        compiler_params=pltpu.CompilerParams(
            collective_id=0, has_side_effects=True, vmem_limit_bytes=67043328
        ),
    )(
        tokens,
        norm_gain,
        query_weight,
        key_matrix,
        value_matrix,
        out_weight,
        query_gain,
        key_gain,
        post_gain,
        jnp.cos(angles),
        jnp.sin(angles),
    )
    return result


def solution(mesh):
    in_specs = (
        P(("seq", "fsdp"), None),
        P(),
        P("seq", "fsdp"),
        P("seq", "fsdp"),
        P("seq", "fsdp"),
        P("seq", "fsdp"),
        P(),
        P(),
        P(),
    )
    out_specs = P(("seq", "fsdp"), None)
    return jax.shard_map(
        on_device, mesh=mesh, in_specs=in_specs, out_specs=out_specs, check_vma=False
    )
```

time: 231 us -> 218 us (0.944)
  Pallas kernels: 220 us -> 212 us
  local copies, waits for them, and re-layouts: 6.21 us -> 3.49 us
    pallas_call x2 -> x1, Pallas kernels: 220 us -> 212 us  [on_device(): pl.pallas_call(functools.partial(layer_kernel, shards, merge), out_shape=...]
    broadcast_in_dim x2 -> x0, local copies, waits for them, and re-layouts: 2.72 us -> none  [the longest x1 1.36 us: on_device(): norm_gain[None, :]]
where the time goes in v2:
time: 218 us; the launch traced here: 217 us
  Pallas kernels  212 us (97%)
  local copies, waits for them, and re-layouts  3.49 us (2%)
    pallas_call x1, Pallas kernels, on_device(): pl.pallas_call(functools.partial(layer_kernel, shards, merge), out_shape=...  212 us

profile of v2, /device:TPU:5, one launch (start us, length us, event | category | flops | bytes accessed | tf_op | source)
XLA Modules:
  0.0 216.9 jit_solution(4191070935614488854)
XLA Ops:
  0.0 1.8 multiply_sine_fusion
  1.8 211.5 %shard_map.91 = (bf16[256,5376]{1,0:T(8,128)(2,1)}, bf16[336,1024]{1,0:T(8,128)(2,1)}) custom-call(bf16[256,5376]{1,0:T(8,128)(2,1)} %tokens_ref.1, f32[5376]{0:T(1024)} %gain_ref.1, bf16[336,1024]{1,0:T(8,128)(2,1)} %query_ref.1, bf16[336,512]{1,0:T(8,128)(2,1)} %key_ref.1, bf16[336,512]{1,0:T(8,128)(2,1)} %value_ref.1, bf16[336,1024]{1,0:T(8,128)(2,1)} %out_ref.1, ...), custom_call_target="tpu_custom_call" | custom-call | tf_op jit(solution)/shard_map/pallas_call | solution.py:676
  213.4 3.5 %copy.11 = bf16[256,5376]{1,0:T(8,128)(2,1)} copy(bf16[256,5376]{1,0:T(8,128)(2,1)} %get-tuple-element.6) | data formatting | bytes 5505024
  (2 shorter events, 0.0 us)

commit v3 on v2

--- a/solution.py
+++ b/solution.py
@@ -1,4 +1,5 @@
 import functools
+import math
 
 import jax
 import jax.numpy as jnp
@@ -117,10 +118,7 @@
     out_ref,
     query_gain_ref,
     key_gain_ref,
-    post_gain_ref,
-    cosine_ref,
-    sine_ref,
-    result_ref,
+    gathered,
     swap_out,
     query_land,
     pair_land,
@@ -134,7 +132,6 @@
     value_window,
     attended,
     projected,
-    gathered,
     cosines,
     sines,
     ring_send,
@@ -153,6 +150,7 @@
     mixed_recv,
     back_send,
     back_recv,
+    home_sem,
     free_sem,
 ):
     ring = Ring(shards, (ring_send, ring_recv, pair_send, pair_recv))
@@ -271,8 +269,13 @@
     key_sum[...] = jnp.zeros_like(key_sum)
     value_sum[...] = jnp.zeros_like(value_sum)
     query_sum[...] = jnp.zeros_like(query_sum)
-    cosines[...] = jnp.concatenate([cosine_ref[...], cosine_ref[...]], axis=1)
-    sines[...] = jnp.concatenate([-sine_ref[...], sine_ref[...]], axis=1)
+    lanes = lax.broadcasted_iota(jnp.int32, (shard_rows, HEAD_SIZE), 1)
+    positions = me * shard_rows + lax.broadcasted_iota(jnp.int32, (shard_rows, HEAD_SIZE), 0)
+    exponents = (lanes % (HEAD_SIZE // 2)).astype(jnp.float32) * (2.0 / HEAD_SIZE)
+    angles = positions.astype(jnp.float32) * jnp.exp(-exponents * math.log(rope_base))
+    cosines[...] = jnp.cos(angles)
+    turn = jnp.sin(angles)
+    sines[...] = jnp.where(lanes < HEAD_SIZE // 2, -turn, turn)
 
     for slot in range(blocks - 1):
         distance = blocks - 1 - slot
@@ -316,13 +319,23 @@
         products(key_sum, 0, pair_land, 0, width, ring.owner(1, step))
         products(value_sum, 0, pair_land, width, width, ring.owner(-1, step))
 
-    def query(step):
-        products(query_sum, 0, query_land, 0, half, ring.owner(1, step))
-        products(query_sum, half, query_land, half, half, ring.owner(-1, step))
-
-    steps(1, chips - 1, lambda step: ring.hop(step, first))
-    ring.hop(0, second, arrive=[])
+    def query(flows, step):
+        column = flows[0][0] // 2 % pieces * wide
+        ring.landed(flows, step)
+        products(query_sum, column, query_land, column, wide, ring.owner(1, step))
+        column += half
+        products(query_sum, column, query_land, column, wide, ring.owner(-1, step))
+
+    early, late = second[:2], second[2:]
+
+    steps(1, chips - 3, lambda step: ring.hop(step, first))
+    ring.hop(chips - 3, first)
+    ring.hop(0, early, arrive=[])
+    ring.hop(chips - 2, first)
+    ring.hop(1, early)
+    ring.hop(0, late, arrive=[])
     ring.hop(chips - 1, first, leave=[])
+    ring.hop(2, early)
     for piece in range(token_pieces - 1):
         token_copy(piece, 1 - group).wait_recv()
     normed_rows(1 - group, 0, part_rows - token_rows)
@@ -406,8 +419,8 @@
             own_copy(swap_out).start()
 
     def second_step(step):
-        ring.hop(step, second)
-        ring.landed(second, step - 1)
+        ring.hop(step + 2, early)
+        ring.hop(step, late)
 
         @pl.when(step == 1)
         def _():
@@ -422,26 +435,46 @@
 
         @pl.when(step == 3)
         def _():
-            query(0)
+            query(early, 0)
             send_keys()
-            steps(1, 3, query)
+            steps(1, 5, lambda step: query(early, step))
+            steps(0, 3, lambda step: query(late, step))
 
         @pl.when(step > 3)
         def _():
-            query(step - 1)
+            query(early, step + 1)
+            query(late, step - 1)
 
         @pl.when(step == 4)
         def _():
             free_slots()
 
-    steps(1, chips - 1, second_step)
-
+    def finish_query(column):
+        def one(head):
+            taken = pl.ds(pl.multiple_of(column + head * HEAD_SIZE, HEAD_SIZE), HEAD_SIZE)
+            queries[:, taken] = turned(
+                query_sum[:, taken],
+                query_gain_ref[...][None, :],
+                cosines[...],
+                sines[...],
+                score_scale * log2_e,
+            ).astype(jnp.bfloat16)
+
+        steps(0, wide // HEAD_SIZE, one)
+
+    steps(1, chips - 3, second_step)
+    ring.hop(chips - 1, early, leave=[])
+    ring.hop(chips - 3, late)
+    query(early, chips - 2)
+    query(late, chips - 4)
+    query(early, chips - 1)
+    finish_query(0)
+    finish_query(half)
+    ring.hop(chips - 2, late)
     pl.semaphore_wait(free_sem, 3)
     own_copy(out_ref).wait()
     ring.hop(0, third, arrive=[], hand=origin)
-    ring.hop(chips - 1, second, leave=[])
-    ring.landed(second, chips - 2)
-    query(chips - 2)
+    query(late, chips - 3)
 
     @pl.when(me >= 2)
     def _():
@@ -451,21 +484,6 @@
             @pl.when(core == 1)
             def _():
                 near_copy(index, part, 0).start()
-
-    ring.landed(second, chips - 1)
-    query(chips - 1)
-
-    def finish_query(head):
-        taken = head_columns(head)
-        queries[:, taken] = turned(
-            query_sum[:, taken],
-            query_gain_ref[...][None, :],
-            cosines[...],
-            sines[...],
-            score_scale * log2_e,
-        ).astype(jnp.bfloat16)
-
-    steps(0, query_heads, finish_query)
 
     for index, part in stacks:
 
@@ -488,7 +506,8 @@
     masks = jnp.concatenate([lower] * sharing, axis=0)
 
     def place_of(unit):
-        head, part = unit // tiles, unit % tiles
+        turn, part = unit // tiles, unit % tiles
+        head = turn % 2 * (heads // 2) + turn // 2
         start = pl.multiple_of(part * tile, tile)
         column = pl.multiple_of(head * head_width, HEAD_SIZE)
         return head, start, column
@@ -553,6 +572,12 @@
             recv_sem=back_recv.at[chip],
             device_id=(me, 1 - group),
             device_id_type=MESH,
+        )
+
+    def home_copy(chip):
+        home = pl.multiple_of(group * part_rows, 16)
+        return pltpu.make_async_copy(
+            projected.at[chip, pl.ds(home, part_rows)], gathered.at[group, chip], home_sem.at[chip]
         )
 
     def project(way, step):
@@ -567,11 +592,16 @@
             for side in range(2)
         ]
         projected[chip] = (parts[0] + parts[1]).astype(jnp.bfloat16)
-        home = pl.multiple_of(group * part_rows, 16)
-        gathered[group, chip] = projected[chip, pl.ds(home, part_rows)]
+        home_copy(chip).start()
         back_copy(chip, group).start()
 
-    steps(0, units, attend_step)
+    steps(0, units // 2, attend_step)
+    ring.hop(chips - 1, late, leave=[])
+    query(late, chips - 2)
+    query(late, chips - 1)
+    finish_query(wide)
+    finish_query(half + wide)
+    steps(units // 2, units, attend_step)
     ring.hop(1, third)
     mixed_copy(units - 1, group).start()
     steps(0, units, lambda unit: mixed_copy(unit, 1 - group).wait_recv())
@@ -595,23 +625,6 @@
     ring.landed(farthest, middle)
     project(1, middle)
     steps(0, chips, lambda chip: back_copy(chip, 1 - group).wait_recv())
-
-    def final(index):
-        start = pl.multiple_of(index * block, block)
-        values = jnp.concatenate(
-            [
-                gathered[side, chip, pl.ds(start, block), :].astype(jnp.float32)
-                for chip in range(chips)
-                for side in range(2)
-            ],
-            axis=1,
-        )
-        mean_square = jnp.mean(values * values, axis=-1, keepdims=True)
-        scaled = values * lax.rsqrt(mean_square + epsilon) * post_gain_ref[...][None, :]
-        added = raw[group, pl.ds(start, block), :].astype(jnp.float32) + scaled
-        result_ref[pl.ds(start, block), :] = added.astype(jnp.bfloat16)
-
-    steps(0, part_rows // block, final)
 
     for index, part in stacks:
 
@@ -639,6 +652,31 @@
     ring.sent(middle, [], farthest)
     steps(0, units, lambda unit: mixed_copy(unit, group).wait_send())
     steps(0, chips, lambda chip: back_copy(chip, group).wait_send())
+    steps(0, chips, lambda chip: home_copy(chip).wait())
+
+
+def final_kernel(gathered_ref, tokens_ref, gain_ref, result_ref):
+    sides, chips, rows, _ = gathered_ref.shape
+    block = 32
+    gain = gain_ref[...][None, :]
+
+    def one(index):
+        span = pl.ds(pl.multiple_of(index * block, block), block)
+        values = jnp.concatenate(
+            [
+                gathered_ref[side, chip, span, :].astype(jnp.float32)
+                for chip in range(chips)
+                for side in range(sides)
+            ],
+            axis=1,
+        )
+        mean_square = jnp.mean(values * values, axis=-1, keepdims=True)
+        scaled = values * lax.rsqrt(mean_square + epsilon) * gain
+        result_ref[span, :] = (tokens_ref[span, :].astype(jnp.float32) + scaled).astype(
+            jnp.bfloat16
+        )
+
+    steps(0, rows // block, one)
 
 
 def on_device(
@@ -664,23 +702,18 @@
     units = heads * copies
     window = WINDOW_LENGTH + shard_rows
 
-    positions = lax.axis_index("seq") * shard_rows + jnp.arange(shard_rows, dtype=jnp.int32)
-    exponents = jnp.arange(HEAD_SIZE // 2, dtype=jnp.float32) * (2.0 / HEAD_SIZE)
-    frequency = jnp.exp(-exponents * jnp.log(jnp.float32(rope_base)))
-    angles = positions.astype(jnp.float32)[:, None] * frequency[None, :]
-
     hbm = pl.BlockSpec(memory_space=pltpu.MemorySpace.HBM)
     vmem = pl.BlockSpec(memory_space=pltpu.VMEM)
     bf16, f32 = jnp.bfloat16, jnp.float32
     dma = pltpu.SemaphoreType.DMA
-    result, _ = pl.pallas_call(
+    gathered, _ = pl.pallas_call(
         functools.partial(layer_kernel, shards, merge),
         out_shape=[
-            jax.ShapeDtypeStruct(tokens.shape, bf16),
+            jax.ShapeDtypeStruct((copies, chips, part_rows, rows), bf16),
             jax.ShapeDtypeStruct(out_weight.shape, bf16),
         ],
-        in_specs=[hbm, vmem, hbm, hbm, hbm, hbm, vmem, vmem, vmem, vmem, vmem],
-        out_specs=[vmem, hbm],
+        in_specs=[hbm, vmem, hbm, hbm, hbm, hbm, vmem, vmem],
+        out_specs=[hbm, hbm],
         scratch_shapes=[
             pltpu.VMEM((shards, rows, query_width), bf16),
             pltpu.VMEM((shards, rows, query_width), bf16),
@@ -694,7 +727,6 @@
             pltpu.VMEM((heads, window, 2 * HEAD_SIZE), bf16),
             pltpu.VMEM((copies, shard_rows, query_width), bf16),
             pltpu.VMEM((chips, shard_rows, rows), bf16),
-            pltpu.VMEM((copies, chips, part_rows, rows), bf16),
             pltpu.VMEM((shard_rows, HEAD_SIZE), f32),
             pltpu.VMEM((shard_rows, HEAD_SIZE), f32),
             *[dma((4 * pieces + 4, chips))] * 4,
@@ -708,6 +740,7 @@
             dma((2,)),
             dma((units,)),
             dma((units,)),
+            dma((chips,)),
             dma((chips,)),
             dma((chips,)),
             pltpu.SemaphoreType.REGULAR,
@@ -724,11 +757,19 @@
         out_weight,
         query_gain,
         key_gain,
-        post_gain,
-        jnp.cos(angles),
-        jnp.sin(angles),
     )
-    return result
+    tile = 64
+    return pl.pallas_call(
+        final_kernel,
+        out_shape=jax.ShapeDtypeStruct(tokens.shape, bf16),
+        grid=(part_rows // tile,),
+        in_specs=[
+            pl.BlockSpec((copies, chips, tile, rows), lambda i: (0, 0, i, 0)),
+            pl.BlockSpec((tile, model_width), lambda i: (i, 0)),
+            pl.BlockSpec((model_width,), lambda i: (0,)),
+        ],
+        out_specs=pl.BlockSpec((tile, model_width), lambda i: (i, 0)),
+    )(gathered, tokens, post_gain)
 
 
 def solution(mesh):

time: 218 us -> 209 us (0.959)
  Pallas kernels: 212 us -> 208 us
  local copies, waits for them, and re-layouts: 3.49 us -> 0 us
    pallas_call x1, Pallas kernels: 212 us -> 202 us  [on_device(): pl.pallas_call(functools.partial(layer_kernel, shards, merge), out_shape=...]
    pallas_call x0 -> x1, Pallas kernels: none -> 6.11 us  [on_device(): pl.pallas_call(final_kernel, out_shape=jax.ShapeDtypeStruct(tokens.shape,...]
    unnamed x1 -> x0, local copies, waits for them, and re-layouts: 3.49 us -> none
where the time goes in v3:
time: 209 us; the launch traced here: 208 us
  Pallas kernels  208 us (100%)
    pallas_call x1, Pallas kernels, on_device(): pl.pallas_call(functools.partial(layer_kernel, shards, merge), out_shape=...  202 us
    pallas_call x1, Pallas kernels, on_device(): pl.pallas_call(final_kernel, out_shape=jax.ShapeDtypeStruct(tokens.shape,...  6.11 us

profile of v3, /device:TPU:5, one launch (start us, length us, event | category | flops | bytes accessed | tf_op | source)
XLA Modules:
  0.0 208.3 jit_solution(6134921244463100154)
XLA Ops:
  0.0 202.2 %shard_map.91 = (bf16[2,8,256,336]{3,2,1,0:T(8,128)(2,1)}, bf16[336,1024]{1,0:T(8,128)(2,1)}) custom-call(bf16[256,5376]{1,0:T(8,128)(2,1)} %tokens_ref.3, f32[5376]{0:T(1024)} %gain_ref.2, bf16[336,1024]{1,0:T(8,128)(2,1)} %query_ref.1, bf16[336,512]{1,0:T(8,128)(2,1)} %key_ref.1, bf16[336,512]{1,0:T(8,128)(2,1)} %value_ref.1, bf16[336,1024]{1,0:T(8,128)(2,1)} %out_ref.1, ...), custom_call_target="tpu_custom_call" | custom-call | tf_op jit(solution)/shard_map/pallas_call | solution.py:709
  202.2 6.1 %shard_map.92 = bf16[256,5376]{1,0:T(8,128)(2,1)} custom-call(bf16[2,8,256,336]{3,2,1,0:T(8,128)(2,1)} %get-tuple-element.6.gathered_ref, bf16[256,5376]{1,0:T(8,128)(2,1)} %tokens_ref.3, f32[5376]{0:T(1024)} %gain_ref.3), custom_call_target="tpu_custom_call" | custom-call | tf_op jit(solution)/shard_map/pallas_call | solution.py:762

commit v4 on v3

--- a/solution.py
+++ b/solution.py
@@ -328,14 +328,16 @@
 
     early, late = second[:2], second[2:]
 
-    steps(1, chips - 3, lambda step: ring.hop(step, first))
+    steps(1, chips - 4, lambda step: ring.hop(step, first))
+    ring.hop(chips - 4, first)
+    ring.hop(0, early, arrive=[])
     ring.hop(chips - 3, first)
-    ring.hop(0, early, arrive=[])
+    ring.hop(1, early)
     ring.hop(chips - 2, first)
-    ring.hop(1, early)
+    ring.hop(2, early)
     ring.hop(0, late, arrive=[])
     ring.hop(chips - 1, first, leave=[])
-    ring.hop(2, early)
+    ring.hop(3, early)
     for piece in range(token_pieces - 1):
         token_copy(piece, 1 - group).wait_recv()
     normed_rows(1 - group, 0, part_rows - token_rows)
@@ -419,7 +421,7 @@
             own_copy(swap_out).start()
 
     def second_step(step):
-        ring.hop(step + 2, early)
+        ring.hop(step + 3, early)
         ring.hop(step, late)
 
         @pl.when(step == 1)
@@ -444,10 +446,6 @@
         def _():
             query(early, step + 1)
             query(late, step - 1)
-
-        @pl.when(step == 4)
-        def _():
-            free_slots()
 
     def finish_query(column):
         def one(head):
@@ -462,14 +460,18 @@
 
         steps(0, wide // HEAD_SIZE, one)
 
-    steps(1, chips - 3, second_step)
+    steps(1, chips - 4, second_step)
     ring.hop(chips - 1, early, leave=[])
-    ring.hop(chips - 3, late)
+    ring.hop(chips - 4, late)
+    query(early, chips - 3)
     query(early, chips - 2)
-    query(late, chips - 4)
     query(early, chips - 1)
     finish_query(0)
     finish_query(half)
+    query(late, chips - 5)
+    free_slots()
+    ring.hop(chips - 3, late)
+    query(late, chips - 4)
     ring.hop(chips - 2, late)
     pl.semaphore_wait(free_sem, 3)
     own_copy(out_ref).wait()
@@ -579,6 +581,19 @@
         return pltpu.make_async_copy(
             projected.at[chip, pl.ds(home, part_rows)], gathered.at[group, chip], home_sem.at[chip]
         )
+
+    def project_rows(chip, side_of_pair):
+        span = pl.ds(pl.multiple_of(side_of_pair * part_rows, 16), part_rows)
+        parts = [
+            lax.dot_general(
+                attended[side, span, :],
+                pair_land[chip * 2 + side],
+                (((1,), (1,)), ((), ())),
+                preferred_element_type=jnp.float32,
+            )
+            for side in range(2)
+        ]
+        projected[chip, span, :] = (parts[0] + parts[1]).astype(jnp.bfloat16)
 
     def project(way, step):
         chip = ring.owner(way, step)
@@ -601,8 +616,9 @@
     query(late, chips - 1)
     finish_query(wide)
     finish_query(half + wide)
+    ring.hop(1, third[:2])
     steps(units // 2, units, attend_step)
-    ring.hop(1, third)
+    ring.hop(1, third[2:])
     mixed_copy(units - 1, group).start()
     steps(0, units, lambda unit: mixed_copy(unit, 1 - group).wait_recv())
     ring.landed(origin, 0)
@@ -623,7 +639,11 @@
     both(middle - 1)
     ring.hop(middle, farthest, leave=[])
     ring.landed(farthest, middle)
-    project(1, middle)
+    last = ring.owner(1, middle)
+    project_rows(last, 1 - group)
+    back_copy(last, group).start()
+    project_rows(last, group)
+    home_copy(last).start()
     steps(0, chips, lambda chip: back_copy(chip, 1 - group).wait_recv())
 
     for index, part in stacks:

time: 209 us -> 208 us (level)
  no operation moved by 1% of the time
where the time goes in v4:
time: 208 us
  Pallas kernels  208 us (100%)
    pallas_call x1, Pallas kernels, on_device(): pl.pallas_call(functools.partial(layer_kernel, shards, merge), out_shape=...  202 us
    pallas_call x1, Pallas kernels, on_device(): pl.pallas_call(final_kernel, out_shape=jax.ShapeDtypeStruct(tokens.shape,...  6.11 us

profile of v4, /device:TPU:5, one launch (start us, length us, event | category | flops | bytes accessed | tf_op | source)
XLA Modules:
  0.0 207.7 jit_solution(3968673816702267838)
XLA Ops:
  0.0 201.5 %shard_map.91 = (bf16[2,8,256,336]{3,2,1,0:T(8,128)(2,1)}, bf16[336,1024]{1,0:T(8,128)(2,1)}) custom-call(bf16[256,5376]{1,0:T(8,128)(2,1)} %tokens_ref.3, f32[5376]{0:T(1024)} %gain_ref.2, bf16[336,1024]{1,0:T(8,128)(2,1)} %query_ref.1, bf16[336,512]{1,0:T(8,128)(2,1)} %key_ref.1, bf16[336,512]{1,0:T(8,128)(2,1)} %value_ref.1, bf16[336,1024]{1,0:T(8,128)(2,1)} %out_ref.1, ...), custom_call_target="tpu_custom_call" | custom-call | tf_op jit(solution)/shard_map/pallas_call | solution.py:729
  201.6 6.1 %shard_map.92 = bf16[256,5376]{1,0:T(8,128)(2,1)} custom-call(bf16[2,8,256,336]{3,2,1,0:T(8,128)(2,1)} %get-tuple-element.6.gathered_ref, bf16[256,5376]{1,0:T(8,128)(2,1)} %tokens_ref.3, f32[5376]{0:T(1024)} %gain_ref.3), custom_call_target="tpu_custom_call" | custom-call | tf_op jit(solution)/shard_map/pallas_call | solution.py:782
